TPU v7x, 256 devices: a whole 4x4x8 slice. The times are simulated.
256 devices in a mesh: gx: 4 (over z_hi), gy: 4 (over y), gz: 16 (over x, z_lo, core).
Axes of the slice: x: 4, y: 4, z: 8 (z_hi: 4, z_lo: 2; z = z_hi * 2 + z_lo), core: 2. Of those that a mesh axis runs over, the one named last changes fastest.
Arguments:
- volume: float32 [256, 256, 4096], P('gz', 'gy', 'gx'), may hold values from -24 to 24
Outputs:
- level_one: float32 [128, 128, 2048], P('gz', 'gy', 'gx')
- level_two: float32 [64, 64, 1024], P('gz', 'gy', 'gx')
- level_three: float32 [32, 32, 512], P('gz', 'gy', 'gx')
All inputs are finite; a program needn't handle non-finite values.
Results may differ from a plain program's by a relative error of at most 0.00002.
Values sent between devices are 32-bit elements; how exact they have to be, the bound alone decides.
No kernel may reach another device: no remote copies, remote signals or barrier semaphores. Data moves between devices by JAX's collectives and lax.ppermute only.
A program may use at most 64 MiB of HBM per device.

v0:
```python
import jax
import jax.numpy as jnp
from jax import lax
from jax.sharding import PartitionSpec as P

taps = (0.0625, 0.25, 0.375, 0.25, 0.0625)


def extended(cells, sides, width):
    for axis, dim in sides:
        count = lax.axis_size(axis)
        ends = count - 1
        head = lax.slice_in_dim(cells, 0, width, axis=dim)
        tail = lax.slice_in_dim(cells, cells.shape[dim] - width, cells.shape[dim], axis=dim)
        cells = jnp.concatenate(
            [
                lax.ppermute(tail, axis, [(i, (i + 1) % count) for i in range(ends)]),
                cells,
                lax.ppermute(head, axis, [((i + 1) % count, i) for i in range(ends)]),
            ],
            axis=dim,
        )
    return cells


def reduce_padded(padded, dim, count):
    total = None
    for k in range(5):
        piece = lax.slice_in_dim(padded, k, k + 2 * count - 1, 2, dim)
        term = taps[k] * piece
        total = term if total is None else total + term
    return total


def pass_sections(block):
    padded = extended(block, (("gz", 0),), 2)
    return reduce_padded(padded, 0, block.shape[0] // 2)


def pass_rows(block):
    padded = extended(block, (("gy", 1),), 2)
    return reduce_padded(padded, 1, block.shape[1] // 2)


def pass_columns(block):
    padded = extended(block, (("gx", 2),), 2)
    return reduce_padded(padded, 2, block.shape[2] // 2)


def level_down(block):
    return pass_columns(pass_rows(pass_sections(block)))


def on_device(volume):
    level_one = level_down(volume)
    level_two = level_down(level_one)
    level_three = level_down(level_two)
    return (level_one, level_two, level_three)


def solution(mesh):
    in_specs = (P("gz", "gy", "gx"),)
    out_specs = (P("gz", "gy", "gx"), P("gz", "gy", "gx"), P("gz", "gy", "gx"))
    return jax.shard_map(
        on_device, mesh=mesh, in_specs=in_specs, out_specs=out_specs, check_vma=False
    )
```

profile of v0, /device:TPU:66, one launch (start us, length us, event | category | flops | bytes accessed | tf_op | source)
XLA Modules:
  0.0 221.4 jit_solution(7761092275039604067)
XLA Ops:
  3.9 4.5 %collective-permute-start.1 = (f32[2,64,1024]{2,1,0:T(8,128)S(1)}, f32[2,64,1024]{2,1,0:T(8,128)S(1)}, u32[]{:S(2)}, u32[]{:S(2)}) collective-permute-start(f32[2,64,1024]{2,1,0:T(8,128)S(1)} %get-tuple-element.3), channel_id=1, source_target_pairs={{1,0},{2,1},{3,2},{4,3},{5,4},{6,5},{7,6},{8,7},{9,8},{10,9},{11,1... | collective-permute-start | bytes 1572872 | tf_op jit(solution)/shard_map/ppermute | solution.py:19
  8.4 7.3 %collective-permute-done = f32[2,64,1024]{2,1,0:T(8,128)S(1)} collective-permute-done((f32[2,64,1024]{2,1,0:T(8,128)S(1)}, f32[2,64,1024]{2,1,0:T(8,128)S(1)}, u32[]{:S(2)}, u32[]{:S(2)}) %collective-permute-start) | collective-permute-done | bytes 524320 | tf_op jit(solution)/shard_map/ppermute | solution.py:17
  15.8 2.7 %constant_dynamic-update-slice_fusion.1 = f32[20,64,1024]{2,1,0:T(8,128)S(1)} fusion(f32[20,64,1024]{2,1,0:T(8,128)S(1)} %constant_dynamic-update-slice_fusion.2, f32[16,64,1024]{2,1,0:T(8,128)} %param.1), kind=kLoop, calls=%fused_computation.16 | loop fusion | bytes 8388608
  20.4 3.5 %collective-permute-start.2 = (f32[8,2,1024]{2,1,0:T(2,128)S(1)}, f32[8,2,1024]{2,1,0:T(2,128)S(1)}, u32[]{:S(2)}, u32[]{:S(2)}) collective-permute-start(f32[8,2,1024]{2,1,0:T(2,128)S(1)} %get-tuple-element.5), channel_id=1, source_target_pairs={{0,16},{16,32},{32,48},{1,17},{17,33},{33,49},{2,18},{18,34},{34,5... | collective-permute-start | bytes 196616 | tf_op jit(solution)/shard_map/ppermute | solution.py:17
  25.6 2.8 %slice.201 = f32[8,32,1024]{2,1,0:T(8,128)} slice(f32[8,64,1024]{2,1,0:T(8,128)S(1)} %multiply_add_fusion), slice={[0:8:1], [1:64:2], [0:1024:1]} | slice | bytes 2097152 | tf_op jit(solution)/shard_map/slice | solution.py:29
  31.8 5.5 %slice.202 = f32[8,32,1024]{2,1,0:T(8,128)} slice(f32[8,68,1024]{2,1,0:T(8,128)} %pad_maximum_fusion), slice={[0:8:1], [4:67:2], [0:1024:1]} | slice | bytes 2097152 | tf_op jit(solution)/shard_map/slice | solution.py:29
  37.2 5.5 %slice.199 = f32[8,32,1024]{2,1,0:T(8,128)} slice(f32[8,68,1024]{2,1,0:T(8,128)} %pad_maximum_fusion), slice={[0:8:1], [1:64:2], [0:1024:1]} | slice | bytes 2097152 | tf_op jit(solution)/shard_map/slice | solution.py:29
  42.8 5.4 %slice.198 = f32[8,32,1024]{2,1,0:T(8,128)} slice(f32[8,68,1024]{2,1,0:T(8,128)} %pad_maximum_fusion), slice={[0:8:1], [0:63:2], [0:1024:1]} | slice | bytes 2097152 | tf_op jit(solution)/shard_map/slice | solution.py:29
  48.1 2.4 %multiply_add_fusion.1 = f32[8,32,1024]{2,1,0:T(8,128)S(1)} fusion(f32[8,32,1024]{2,1,0:T(8,128)} %slice.202, f32[8,32,1024]{2,1,0:T(8,128)S(1)} %copy-done.2, f32[8,32,1024]{2,1,0:T(8,128)S(1)} %slice.200, f32[8,32,1024]{2,1,0:T(8,128)} %slice.199, f32[8,32,1024]{2,1,0:T(8,128)} %slice.198), kind=kLoop, calls=%fused_computation.2 | loop fusion | flops 2359296 | bytes 6291456 | tf_op jit(solution)/shard_map/add | solution.py:31
  52.6 7.5 %collective-permute-start.4 = (f32[8,32,2]{2,1,0:T(8,128)S(1)}, f32[8,32,2]{2,1,0:T(8,128)S(1)}, u32[]{:S(2)}, u32[]{:S(2)}) collective-permute-start(f32[8,32,2]{2,1,0:T(8,128)S(1)} %get-tuple-element.8), channel_id=1, source_target_pairs={{0,64},{64,128},{128,192},{1,65},{65,129},{129,193},{2,66},{66,130... | collective-permute-start | bytes 6152 | tf_op jit(solution)/shard_map/ppermute | solution.py:17
  60.1 17.6 %slice.207 = f32[8,32,512]{2,1,0:T(8,128)S(1)} slice(f32[8,32,1024]{2,1,0:T(8,128)S(1)} %multiply_add_fusion.1), slice={[0:8:1], [0:32:1], [0:1023:2]} | slice | bytes 1048576 | tf_op jit(solution)/shard_map/slice | solution.py:29
  77.7 17.6 %slice.208 = f32[8,32,512]{2,1,0:T(8,128)S(1)} slice(f32[8,32,1024]{2,1,0:T(8,128)S(1)} %multiply_add_fusion.1), slice={[0:8:1], [0:32:1], [1:1024:2]} | slice | bytes 1048576 | tf_op jit(solution)/shard_map/slice | solution.py:29
  96.1 17.6 %slice.209 = f32[8,32,512]{2,1,0:T(8,128)S(1)} slice(f32[8,32,1028]{2,1,0:T(8,128)S(1)} %concatenate.29), slice={[0:8:1], [0:32:1], [4:1027:2]} | slice | bytes 1048576 | tf_op jit(solution)/shard_map/slice | solution.py:29
  113.7 18.4 %slice.206 = f32[8,32,512]{2,1,0:T(8,128)} slice(f32[8,32,1028]{2,1,0:T(8,128)S(1)} %concatenate.29), slice={[0:8:1], [0:32:1], [1:1024:2]} | slice | bytes 1048576 | tf_op jit(solution)/shard_map/slice | solution.py:29
  132.0 18.2 %slice.205 = f32[8,32,512]{2,1,0:T(8,128)} slice(f32[8,32,1028]{2,1,0:T(8,128)S(1)} %concatenate.29), slice={[0:8:1], [0:32:1], [0:1023:2]} | slice | bytes 1048576 | tf_op jit(solution)/shard_map/slice | solution.py:29
  153.7 4.5 %collective-permute-start.7 = (f32[2,32,512]{2,1,0:T(8,128)S(1)}, f32[2,32,512]{2,1,0:T(8,128)S(1)}, u32[]{:S(2)}, u32[]{:S(2)}) collective-permute-start(f32[2,32,512]{2,1,0:T(8,128)S(1)} %get-tuple-element.10), channel_id=1, source_target_pairs={{1,0},{2,1},{3,2},{4,3},{5,4},{6,5},{7,6},{8,7},{9,8},{10,9},{11,1... | collective-permute-start | bytes 393224 | tf_op jit(solution)/shard_map/ppermute | solution.py:19
  160.9 3.5 %collective-permute-start.8 = (f32[4,2,512]{2,1,0:T(2,128)S(1)}, f32[4,2,512]{2,1,0:T(2,128)S(1)}, u32[]{:S(2)}, u32[]{:S(2)}) collective-permute-start(f32[4,2,512]{2,1,0:T(2,128)S(1)} %get-tuple-element.11), channel_id=1, source_target_pairs={{0,16},{16,32},{32,48},{1,17},{17,33},{33,49},{2,18},{18,34},{34,5... | collective-permute-start | bytes 49160 | tf_op jit(solution)/shard_map/ppermute | solution.py:17
  165.9 4.2 %collective-permute-done.9 = f32[4,2,512]{2,1,0:T(2,128)S(1)} collective-permute-done((f32[4,2,512]{2,1,0:T(2,128)S(1)}, f32[4,2,512]{2,1,0:T(2,128)S(1)}, u32[]{:S(2)}, u32[]{:S(2)}) %collective-permute-start.9) | collective-permute-done | bytes 16416 | tf_op jit(solution)/shard_map/ppermute | solution.py:19
  170.4 4.8 %collective-permute-start.10 = (f32[4,16,2]{2,1,0:T(8,128)S(1)}, f32[4,16,2]{2,1,0:T(8,128)S(1)}, u32[]{:S(2)}, u32[]{:S(2)}) collective-permute-start(f32[4,16,2]{2,1,0:T(8,128)S(1)} %get-tuple-element.13), channel_id=1, source_target_pairs={{0,64},{64,128},{128,192},{1,65},{65,129},{129,193},{2,66},{66,130... | collective-permute-start | bytes 1544 | tf_op jit(solution)/shard_map/ppermute | solution.py:17
  175.2 2.2 collective-permute-start.11
  177.4 2.2 slice.228
  179.7 2.2 slice.229
  183.6 2.2 %slice.230 = f32[4,16,256]{2,1,0:T(8,128)S(1)} slice(f32[4,16,516]{2,1,0:T(8,128)S(1)} %pad_maximum_fusion.3), slice={[0:4:1], [0:16:1], [4:515:2]} | slice | bytes 131072 | tf_op jit(solution)/shard_map/slice | solution.py:29
  185.8 2.2 slice.227
  188.0 2.2 slice.226
  190.3 1.9 collective-permute-start.12
  192.2 4.5 %collective-permute-start.13 = (f32[2,16,256]{2,1,0:T(8,128)S(1)}, f32[2,16,256]{2,1,0:T(8,128)S(1)}, u32[]{:S(2)}, u32[]{:S(2)}) collective-permute-start(f32[2,16,256]{2,1,0:T(8,128)S(1)} %get-tuple-element.16), channel_id=1, source_target_pairs={{1,0},{2,1},{3,2},{4,3},{5,4},{6,5},{7,6},{8,7},{9,8},{10,9},{11,1... | collective-permute-start | bytes 98312 | tf_op jit(solution)/shard_map/ppermute | solution.py:19
  198.4 3.2 %collective-permute-start.14 = (f32[2,2,256]{2,1,0:T(2,128)S(1)}, f32[2,2,256]{2,1,0:T(2,128)S(1)}, u32[]{:S(2)}, u32[]{:S(2)}) collective-permute-start(f32[2,2,256]{2,1,0:T(2,128)S(1)} %get-tuple-element.17), channel_id=1, source_target_pairs={{0,16},{16,32},{32,48},{1,17},{17,33},{33,49},{2,18},{18,34},{34,5... | collective-permute-start | bytes 12296 | tf_op jit(solution)/shard_map/ppermute | solution.py:17
  202.9 4.2 %collective-permute-done.15 = f32[2,2,256]{2,1,0:T(2,128)S(1)} collective-permute-done((f32[2,2,256]{2,1,0:T(2,128)S(1)}, f32[2,2,256]{2,1,0:T(2,128)S(1)}, u32[]{:S(2)}, u32[]{:S(2)}) %collective-permute-start.15) | collective-permute-done | bytes 4128 | tf_op jit(solution)/shard_map/ppermute | solution.py:19
  207.6 4.5 %collective-permute-start.16 = (f32[2,8,2]{2,1,0:T(8,128)S(1)}, f32[2,8,2]{2,1,0:T(8,128)S(1)}, u32[]{:S(2)}, u32[]{:S(2)}) collective-permute-start(f32[2,8,2]{2,1,0:T(8,128)S(1)} %get-tuple-element.19), channel_id=1, source_target_pairs={{0,64},{64,128},{128,192},{1,65},{65,129},{129,193},{2,66},{66,130... | collective-permute-start | bytes 392 | tf_op jit(solution)/shard_map/ppermute | solution.py:17
  212.1 2.3 %collective-permute-start.17 = (f32[2,8,2]{2,1,0:T(8,128)S(1)}, f32[2,8,2]{2,1,0:T(8,128)S(1)}, u32[]{:S(2)}, u32[]{:S(2)}) collective-permute-start(f32[2,8,2]{2,1,0:T(8,128)S(1)} %get-tuple-element.20), channel_id=1, source_target_pairs={{64,0},{128,64},{192,128},{65,1},{129,65},{193,129},{66,2},{130,66... | collective-permute-start | bytes 392 | tf_op jit(solution)/shard_map/ppermute | solution.py:19
  214.7 5.0 %collective-permute-done.17 = f32[2,8,2]{2,1,0:T(8,128)S(1)} collective-permute-done((f32[2,8,2]{2,1,0:T(8,128)S(1)}, f32[2,8,2]{2,1,0:T(8,128)S(1)}, u32[]{:S(2)}, u32[]{:S(2)}) %collective-permute-start.17) | collective-permute-done | bytes 160 | tf_op jit(solution)/shard_map/ppermute | solution.py:19
  (71 shorter events, 28.0 us)
Async XLA Ops:
  1.9 13.8 %collective-permute-start = (f32[2,64,1024]{2,1,0:T(8,128)S(1)}, f32[2,64,1024]{2,1,0:T(8,128)S(1)}, u32[]{:S(2)}, u32[]{:S(2)}) collective-permute-start(f32[2,64,1024]{2,1,0:T(8,128)S(1)} %get-tuple-element.4), channel_id=1, source_target_pairs={{0,1},{1,2},{2,3},{3,4},{4,5},{5,6},{6,7},{7,8},{8,9},{9,10},{10,1... | collective-permute-start | bytes 1572872 | tf_op jit(solution)/shard_map/ppermute | solution.py:17
  3.9 14.6 %collective-permute-start.1 = (f32[2,64,1024]{2,1,0:T(8,128)S(1)}, f32[2,64,1024]{2,1,0:T(8,128)S(1)}, u32[]{:S(2)}, u32[]{:S(2)}) collective-permute-start(f32[2,64,1024]{2,1,0:T(8,128)S(1)} %get-tuple-element.3), channel_id=1, source_target_pairs={{1,0},{2,1},{3,2},{4,3},{5,4},{6,5},{7,6},{8,7},{9,8},{10,9},{11,1... | collective-permute-start | bytes 1572872 | tf_op jit(solution)/shard_map/ppermute | solution.py:19
  15.8 3.5 %copy-start = (f32[16,64,1024]{2,1,0:T(8,128)S(1)}, f32[16,64,1024]{2,1,0:T(8,128)}, u32[]{:S(2)}) copy-start(f32[16,64,1024]{2,1,0:T(8,128)} %param.1) | copy-start | bytes 12582916
  20.4 8.1 %collective-permute-start.2 = (f32[8,2,1024]{2,1,0:T(2,128)S(1)}, f32[8,2,1024]{2,1,0:T(2,128)S(1)}, u32[]{:S(2)}, u32[]{:S(2)}) collective-permute-start(f32[8,2,1024]{2,1,0:T(2,128)S(1)} %get-tuple-element.5), channel_id=1, source_target_pairs={{0,16},{16,32},{32,48},{1,17},{17,33},{33,49},{2,18},{18,34},{34,5... | collective-permute-start | bytes 196616 | tf_op jit(solution)/shard_map/ppermute | solution.py:17
  23.8 6.2 %collective-permute-start.3 = (f32[8,2,1024]{2,1,0:T(2,128)S(1)}, f32[8,2,1024]{2,1,0:T(2,128)S(1)}, u32[]{:S(2)}, u32[]{:S(2)}) collective-permute-start(f32[8,2,1024]{2,1,0:T(2,128)S(1)} %get-tuple-element.6), channel_id=1, source_target_pairs={{16,0},{32,16},{48,32},{17,1},{33,17},{49,33},{18,2},{34,18},{50,3... | collective-permute-start | bytes 196616 | tf_op jit(solution)/shard_map/ppermute | solution.py:19
  37.2 10.9 %copy-start.2 = (f32[8,32,1024]{2,1,0:T(8,128)S(1)}, f32[8,32,1024]{2,1,0:T(8,128)}, u32[]{:S(2)}) copy-start(f32[8,32,1024]{2,1,0:T(8,128)} %slice.201) | copy-start | bytes 3145732
  50.7 44.6 %collective-permute-start.5 = (f32[8,32,2]{2,1,0:T(8,128)S(1)}, f32[8,32,2]{2,1,0:T(8,128)S(1)}, u32[]{:S(2)}, u32[]{:S(2)}) collective-permute-start(f32[8,32,2]{2,1,0:T(8,128)S(1)} %get-tuple-element.7), channel_id=1, source_target_pairs={{64,0},{128,64},{192,128},{65,1},{129,65},{193,129},{66,2},{130,66... | collective-permute-start | bytes 6152 | tf_op jit(solution)/shard_map/ppermute | solution.py:19
  52.6 42.6 %collective-permute-start.4 = (f32[8,32,2]{2,1,0:T(8,128)S(1)}, f32[8,32,2]{2,1,0:T(8,128)S(1)}, u32[]{:S(2)}, u32[]{:S(2)}) collective-permute-start(f32[8,32,2]{2,1,0:T(8,128)S(1)} %get-tuple-element.8), channel_id=1, source_target_pairs={{0,64},{64,128},{128,192},{1,65},{65,129},{129,193},{2,66},{66,130... | collective-permute-start | bytes 6152 | tf_op jit(solution)/shard_map/ppermute | solution.py:17
  151.7 14.1 %copy-start.1 = (f32[8,32,512]{2,1,0:T(8,128)}, f32[8,32,512]{2,1,0:T(8,128)S(1)}, u32[]{:S(2)}) copy-start(f32[8,32,512]{2,1,0:T(8,128)S(1)} %multiply_add_fusion.2) | copy-start | bytes 1572868
  151.7 8.2 %collective-permute-start.6 = (f32[2,32,512]{2,1,0:T(8,128)S(1)}, f32[2,32,512]{2,1,0:T(8,128)S(1)}, u32[]{:S(2)}, u32[]{:S(2)}) collective-permute-start(f32[2,32,512]{2,1,0:T(8,128)S(1)} %get-tuple-element.9), channel_id=1, source_target_pairs={{0,1},{1,2},{2,3},{3,4},{4,5},{5,6},{6,7},{7,8},{8,9},{9,10},{10,1... | collective-permute-start | bytes 393224 | tf_op jit(solution)/shard_map/ppermute | solution.py:17
  153.7 7.0 %collective-permute-start.7 = (f32[2,32,512]{2,1,0:T(8,128)S(1)}, f32[2,32,512]{2,1,0:T(8,128)S(1)}, u32[]{:S(2)}, u32[]{:S(2)}) collective-permute-start(f32[2,32,512]{2,1,0:T(8,128)S(1)} %get-tuple-element.10), channel_id=1, source_target_pairs={{1,0},{2,1},{3,2},{4,3},{5,4},{6,5},{7,6},{8,7},{9,8},{10,9},{11,1... | collective-permute-start | bytes 393224 | tf_op jit(solution)/shard_map/ppermute | solution.py:19
  160.9 4.9 %collective-permute-start.8 = (f32[4,2,512]{2,1,0:T(2,128)S(1)}, f32[4,2,512]{2,1,0:T(2,128)S(1)}, u32[]{:S(2)}, u32[]{:S(2)}) collective-permute-start(f32[4,2,512]{2,1,0:T(2,128)S(1)} %get-tuple-element.11), channel_id=1, source_target_pairs={{0,16},{16,32},{32,48},{1,17},{17,33},{33,49},{2,18},{18,34},{34,5... | collective-permute-start | bytes 49160 | tf_op jit(solution)/shard_map/ppermute | solution.py:17
  164.4 5.6 %collective-permute-start.9 = (f32[4,2,512]{2,1,0:T(2,128)S(1)}, f32[4,2,512]{2,1,0:T(2,128)S(1)}, u32[]{:S(2)}, u32[]{:S(2)}) collective-permute-start(f32[4,2,512]{2,1,0:T(2,128)S(1)} %get-tuple-element.12), channel_id=1, source_target_pairs={{16,0},{32,16},{48,32},{17,1},{33,17},{49,33},{18,2},{34,18},{50,3... | collective-permute-start | bytes 49160 | tf_op jit(solution)/shard_map/ppermute | solution.py:19
  170.4 11.4 %collective-permute-start.10 = (f32[4,16,2]{2,1,0:T(8,128)S(1)}, f32[4,16,2]{2,1,0:T(8,128)S(1)}, u32[]{:S(2)}, u32[]{:S(2)}) collective-permute-start(f32[4,16,2]{2,1,0:T(8,128)S(1)} %get-tuple-element.13), channel_id=1, source_target_pairs={{0,64},{64,128},{128,192},{1,65},{65,129},{129,193},{2,66},{66,130... | collective-permute-start | bytes 1544 | tf_op jit(solution)/shard_map/ppermute | solution.py:17
  175.2 8.2 %collective-permute-start.11 = (f32[4,16,2]{2,1,0:T(8,128)S(1)}, f32[4,16,2]{2,1,0:T(8,128)S(1)}, u32[]{:S(2)}, u32[]{:S(2)}) collective-permute-start(f32[4,16,2]{2,1,0:T(8,128)S(1)} %get-tuple-element.14), channel_id=1, source_target_pairs={{64,0},{128,64},{192,128},{65,1},{129,65},{193,129},{66,2},{130,66... | collective-permute-start | bytes 1544 | tf_op jit(solution)/shard_map/ppermute | solution.py:19
  190.3 31.2 %copy-start.3 = (f32[4,16,256]{2,1,0:T(8,128)}, f32[4,16,256]{2,1,0:T(8,128)S(1)}, u32[]{:S(2)}) copy-start(f32[4,16,256]{2,1,0:T(8,128)S(1)} %multiply_add_fusion.5) | copy-start | bytes 196612
  190.3 6.5 %collective-permute-start.12 = (f32[2,16,256]{2,1,0:T(8,128)S(1)}, f32[2,16,256]{2,1,0:T(8,128)S(1)}, u32[]{:S(2)}, u32[]{:S(2)}) collective-permute-start(f32[2,16,256]{2,1,0:T(8,128)S(1)} %get-tuple-element.15), channel_id=1, source_target_pairs={{0,1},{1,2},{2,3},{3,4},{4,5},{5,6},{6,7},{7,8},{8,9},{9,10},{10,1... | collective-permute-start | bytes 98312 | tf_op jit(solution)/shard_map/ppermute | solution.py:17
  192.2 6.1 %collective-permute-start.13 = (f32[2,16,256]{2,1,0:T(8,128)S(1)}, f32[2,16,256]{2,1,0:T(8,128)S(1)}, u32[]{:S(2)}, u32[]{:S(2)}) collective-permute-start(f32[2,16,256]{2,1,0:T(8,128)S(1)} %get-tuple-element.16), channel_id=1, source_target_pairs={{1,0},{2,1},{3,2},{4,3},{5,4},{6,5},{7,6},{8,7},{9,8},{10,9},{11,1... | collective-permute-start | bytes 98312 | tf_op jit(solution)/shard_map/ppermute | solution.py:19
  198.4 4.5 %collective-permute-start.14 = (f32[2,2,256]{2,1,0:T(2,128)S(1)}, f32[2,2,256]{2,1,0:T(2,128)S(1)}, u32[]{:S(2)}, u32[]{:S(2)}) collective-permute-start(f32[2,2,256]{2,1,0:T(2,128)S(1)} %get-tuple-element.17), channel_id=1, source_target_pairs={{0,16},{16,32},{32,48},{1,17},{17,33},{33,49},{2,18},{18,34},{34,5... | collective-permute-start | bytes 12296 | tf_op jit(solution)/shard_map/ppermute | solution.py:17
  201.6 5.5 %collective-permute-start.15 = (f32[2,2,256]{2,1,0:T(2,128)S(1)}, f32[2,2,256]{2,1,0:T(2,128)S(1)}, u32[]{:S(2)}, u32[]{:S(2)}) collective-permute-start(f32[2,2,256]{2,1,0:T(2,128)S(1)} %get-tuple-element.18), channel_id=1, source_target_pairs={{16,0},{32,16},{48,32},{17,1},{33,17},{49,33},{18,2},{34,18},{50,3... | collective-permute-start | bytes 12296 | tf_op jit(solution)/shard_map/ppermute | solution.py:19
  207.6 7.1 %collective-permute-start.16 = (f32[2,8,2]{2,1,0:T(8,128)S(1)}, f32[2,8,2]{2,1,0:T(8,128)S(1)}, u32[]{:S(2)}, u32[]{:S(2)}) collective-permute-start(f32[2,8,2]{2,1,0:T(8,128)S(1)} %get-tuple-element.19), channel_id=1, source_target_pairs={{0,64},{64,128},{128,192},{1,65},{65,129},{129,193},{2,66},{66,130... | collective-permute-start | bytes 392 | tf_op jit(solution)/shard_map/ppermute | solution.py:17
  212.1 7.7 %collective-permute-start.17 = (f32[2,8,2]{2,1,0:T(8,128)S(1)}, f32[2,8,2]{2,1,0:T(8,128)S(1)}, u32[]{:S(2)}, u32[]{:S(2)}) collective-permute-start(f32[2,8,2]{2,1,0:T(8,128)S(1)} %get-tuple-element.20), channel_id=1, source_target_pairs={{64,0},{128,64},{192,128},{65,1},{129,65},{193,129},{66,2},{130,66... | collective-permute-start | bytes 392 | tf_op jit(solution)/shard_map/ppermute | solution.py:19
where the time goes:
time: 222 us; the launch traced here: 221 us
  local copies, waits for them, and re-layouts  128 us (58%)
  starting transfers between devices  56.5 us (25%)
  waiting for transfers between devices  27.9 us (13%)
  other arithmetic  7.92 us (4%)
    slice x30, local copies, waits for them, and re-layouts, reduce_padded(): piece = lax.slice_in_dim(padded, k, k + 2 * count - 1, 2, dim)  122 us
    ppermute x9, starting transfers between devices, extended(): lax.ppermute(tail, axis, [(i, (i + 1) % count) for i in range(ends)])  32.7 us
    ppermute x9, starting transfers between devices, extended(): lax.ppermute(head, axis, [((i + 1) % count, i) for i in range(ends)])  23.9 us
    ppermute x9, waiting for transfers between devices, extended(): lax.ppermute(head, axis, [((i + 1) % count, i) for i in range(ends)])  18.8 us
    ppermute x9, waiting for transfers between devices, extended(): lax.ppermute(tail, axis, [(i, (i + 1) % count) for i in range(ends)])  9.09 us
    add x9, other arithmetic, reduce_padded(): total = term if total is None else total + term  5.86 us
  transfers between devices with their start and end apart: 18, of which 9 were waited for; matrix products, arithmetic and copies ran while one was open for 21% of the time, Pallas kernels for 0%

commit v1 on v0

v1 whole, which is shorter than its diff:
```python
import numpy as np
import jax
import jax.numpy as jnp
from jax import lax
from jax.experimental import pallas as pl
from jax.experimental.pallas import tpu as pltpu
from jax.sharding import PartitionSpec as P

taps = (0.0625, 0.25, 0.375, 0.25, 0.0625)
f32, bf16 = jnp.float32, jnp.bfloat16
VMEM = pl.BlockSpec(memory_space=pltpu.VMEM)


def column_weights():
    w = np.zeros((256, 256), np.float32)
    for i in range(-1, 129):
        for k in range(5):
            c = 2 * i - 2 + k
            if 0 <= c < 256:
                lane = i if 0 <= i < 128 else (128 if i == 128 else 255)
                w[c, lane] += taps[k]
    return np.concatenate([w] * 3, axis=0)


def edge_weights():
    w = np.zeros((128, 256), np.float32)
    for c in range(128):
        for k in range(5):
            place = c - 128 if c >= 64 else c
            if (place + 2 - k) % 2:
                continue
            i = (place + 2 - k) // 2
            if c >= 64:
                lane = 128 + i if i < 0 else 128 + i
                w[c, lane] += taps[k]
            else:
                lane = i if i >= 0 else 256 + i
                w[c, lane] += taps[k]
    return np.concatenate([w] * 3, axis=0)


def composite(levels):
    h = np.ones(1)
    for level in range(levels):
        up = np.zeros(4 * 2**level + 1)
        up[:: 2**level] = taps
        h = np.convolve(h, up)
    return h


def shell_weights():
    rows = [(1, 0), (2, 0), (2, 1), (3, 0), (3, 1), (1, -1), (2, -1), (3, -1)]
    w = np.zeros((8, 256), np.float64)
    for r, (level, place) in enumerate(rows):
        h = composite(level)
        reach = len(h) // 2
        for t in range(len(h)):
            c = place * 2**level + t - reach
            if r < 5 and -128 <= c < 0:
                w[r, 256 + c] = h[t]
            if r >= 5 and 0 <= c < 128:
                w[r, c] = h[t]
    high = w.astype(jnp.bfloat16).astype(np.float64)
    return np.concatenate([high, w - high], axis=0).astype(np.float32)


def split(x):
    a = x.astype(bf16)
    r = x - a.astype(f32)
    b = r.astype(bf16)
    return a, b, (r - b.astype(f32)).astype(bf16)


def weigh(p):
    total = None
    for a, b, t in ((p[0], p[4], taps[0]), (p[1], p[3], taps[1]), (p[2], None, taps[2])):
        if a is None and b is None:
            continue
        s = a if b is None else b if a is None else a + b
        total = t * s if total is None else total + t * s
    return total


def keep(axis, count):
    at = lax.axis_index(axis)
    return (
        jnp.where(at > 0, 1.0, 0.0).astype(f32),
        jnp.where(at < count - 1, 1.0, 0.0).astype(f32),
    )


def sections(load, store, first, last, half, above, ends):
    got = {i: load(i) for i in range(first, last + 1)}
    for i in range(-1, half + above):
        v = weigh([got.get(2 * i - 2 + k) for k in range(5)])
        if i < 0:
            v = v * ends[0]
        if i >= half:
            v = v * ends[1]
        store(i, v)


def rows(src, dst, at, half, above, ends):
    n = 2 * half
    dst[at, 8 : 8 + half, :] = weigh(
        [src[at, pl.ds(6 + k, half, stride=2), :] for k in range(5)]
    )
    low = taps[3] * src[at, 7:8, :] + taps[4] * src[at, 8:9, :]
    dst[at, 0:8, :] = jnp.where(
        lax.broadcasted_iota(jnp.int32, (8, 128), 0) == 7, low * ends[0], 0.0
    )
    up = [src[at, 6 + n + k : 7 + n + k, :] for k in range(4)]
    high = weigh(up + [None]) * ends[1]
    higher = (taps[0] * up[2] + taps[1] * up[3]) * ends[1]
    row = lax.broadcasted_iota(jnp.int32, (8, 128), 0)
    dst[at, 8 + half : 16 + half, :] = jnp.where(row == 0, high, jnp.where(row == 1, higher, 0.0))


def pack(parts, dst, at):
    wide = len(parts) * 128
    tall = parts[0].shape[0]
    for j, x in enumerate(parts):
        for q, piece in enumerate(split(x)):
            dst[at : at + tall, q * wide + j * 128 : q * wide + (j + 1) * 128] = piece


def lane():
    return lax.broadcasted_iota(jnp.int32, (8, 128), 1)


def low_lanes(tall):
    return lax.broadcasted_iota(jnp.int32, (tall, 128), 1) < 64


def matmul(x, w):
    return jnp.dot(x, w, preferred_element_type=f32)


def shell_kernel(left, right, w, out):
    x = jnp.concatenate([left[...].reshape(1024, 128), right[...].reshape(1024, 128)], axis=1)
    total = None
    for piece in split(x):
        t = lax.dot_general(w[...], piece, (((1,), (1,)), ((), ())), preferred_element_type=f32)
        total = t if total is None else total + t
    out[...] = total[:8] + total[8:]


def level_one_block(volume, at, zs, ys, ops, res, w, zend, yend):
    for h in range(2):
        cols = pl.ds(at * 256 + h * 128, 128)
        for s in range(10):
            zs[h, s, 0:8, :] = jnp.zeros((8, 128), f32)
            zs[h, s, 72:80, :] = jnp.zeros((8, 128), f32)
        for r in range(0, 64, 8):

            def store(i, v, r=r, h=h):
                zs[h, i + 1, 8 + r : 16 + r, :] = v

            sections(lambda i, r=r, cols=cols: volume[i, r : r + 8, cols], store, 0, 15, 8, 1, zend)
    for s in range(10):
        for h in range(2):
            rows(zs.at[h], ys.at[h], s, 32, 1, yend)
        pack([ys[0, s], ys[1, s]], ops, s * 48)
    res[...] = matmul(ops[...], w[...])


def first_kernel(volume, w, ea, side, zs, ys, ops, res):
    zend, yend = keep("gz", lax.axis_size("gz")), keep("gy", lax.axis_size("gy"))
    low = low_lanes(48)
    for b in range(2):
        level_one_block(volume, b, zs, ys, ops, res, w, zend, yend)
        for s in range(10):
            main = res[s * 48 : s * 48 + 48, :128]
            beside = res[s * 48 : s * 48 + 48, 128:]
            if b == 0:
                ea[0, s] = main
                side[s] = beside
            else:
                first = side[s]
                ea[1, s] = main + jnp.where(low, first, 0.0)
                ea[0, s] = ea[0, s] + jnp.where(low, 0.0, beside)
                side[s] = jnp.where(low, beside, first)


def next_level(blocks, edge, zs, ys, ops, edge_ops, res, edge_res, w, we, dst, edge_dst,
               sections_in, half_z, half_y, tall_in, used_in, tall, zend, yend, xend):
    count = len(blocks)
    many = half_z + 3
    for j, src in enumerate(blocks + [edge]):
        for r in range(0, used_in, 8):

            def store(i, v, r=r, j=j):
                zs[j, i + 1, r : r + 8, :] = v

            sections(lambda i, r=r, src=src: src[i + 1, r : r + 8, :], store, -1,
                     sections_in - 2, half_z, 2, zend)
        for s in range(many):
            rows(zs.at[j], ys.at[j], s, half_y, 2, yend)
    size = many * tall
    for p in range(count // 2):
        for s in range(many):
            pack([ys[2 * p, s], ys[2 * p + 1, s]], ops, p * size + s * tall)
    for s in range(many):
        pack([ys[count, s]], edge_ops, s * tall)
    res[...] = matmul(ops[...], w[...])
    edge_res[...] = matmul(edge_ops[...], we[...])
    low = low_lanes(tall)
    last = count // 2 - 1
    for s in range(many):
        mains, besides = [], []
        for p in range(last + 1):
            at = p * size + s * tall
            mains.append(res[at : at + tall, :128])
            besides.append(res[at : at + tall, 128:])
        at = s * tall
        edge_beside = edge_res[at : at + tall, 128:]
        for p in range(last + 1):
            under = besides[p - 1] if p else edge_beside
            over = besides[p + 1] if p < last else edge_beside
            dst[p, s] = mains[p] + jnp.where(low, under, over)
        if edge_dst is not None:
            wrapped = edge_res[at : at + tall, :128] + jnp.where(low, besides[last], besides[0])
            edge_dst[s] = wrapped * jnp.where(low, xend[1], xend[0])


def second_kernel(volume, w, we, ea_in, side, ea, eb, f2, f3,
                  zs, ys, ops, res, h1, z2, y2, ops2, opse2, res2, rese2, h2,
                  z3, y3, ops3, opse3, res3, rese3):
    zend, yend, xend = (keep(a, lax.axis_size(a)) for a in ("gz", "gy", "gx"))
    low = low_lanes(48)
    ea[0] = ea_in[0]
    for b in range(2):
        level_one_block(volume, 2 + b, zs, ys, ops, res, w, zend, yend)
        for s in range(10):
            main = res[s * 48 : s * 48 + 48, :128]
            beside = res[s * 48 : s * 48 + 48, 128:]
            if b == 0:
                eb[0, s] = main + jnp.where(low, side[s], 0.0)
                ea[1, s] = ea_in[1, s] + jnp.where(low, 0.0, beside)
                h1[s] = beside
            else:
                eb[1, s] = main + jnp.where(low, h1[s], 0.0)
                eb[0, s] = eb[0, s] + jnp.where(low, 0.0, beside)
                h1[s] = jnp.where(low, beside * xend[1], side[s] * xend[0])
    next_level([ea.at[0], ea.at[1], eb.at[0], eb.at[1]], h1, z2, y2, ops2, opse2, res2, rese2,
               w, we, f2, h2, 10, 4, 16, 48, 48, 32, zend, yend, xend)
    next_level([f2.at[0], f2.at[1]], h2, z3, y3, ops3, opse3, res3, rese3,
               w, we, f3, None, 7, 2, 8, 32, 32, 32, zend, yend, xend)


def route(x, base, tall):
    at = lax.broadcasted_iota(jnp.int32, (tall, 128), 1)
    first, count, last = base
    head = x if first == 0 else pltpu.roll(x, 128 - first, axis=1)
    tail = pltpu.roll(x, 127 - last, axis=1)
    return jnp.where(at < count, head, 0.0), jnp.where(at == 127, tail, 0.0)


def columns_kernel(pa, pb, ea_in, eb_in, f2_in, f3_in, ea, eb, f2, f3, ya, yb,
                   flat, zs, y1, z2, y2, z3, y3):
    zend, yend = keep("gz", lax.axis_size("gz")), keep("gy", lax.axis_size("gy"))
    odd = lax.rem(lax.axis_index("gx"), 2) == 1
    row = lax.broadcasted_iota(jnp.int32, (8, 128), 0)
    for j in range(8):
        a, b = pa[:, j * 128 : j * 128 + 128], pb[:, j * 128 : j * 128 + 128]
        under, over = jnp.where(odd, a, b), jnp.where(odd, b, a)
        mine = jnp.where(row < 5, under, over)
        full = jnp.concatenate([mine, jnp.zeros((120, 128), f32)], axis=0)
        flat[2 * j : 2 * j + 2] = full.T.reshape(2, 64, 128)
    for s in range(10):
        zs[s, 0:8, :] = jnp.zeros((8, 128), f32)
        zs[s, 72:80, :] = jnp.zeros((8, 128), f32)
    for r in range(0, 64, 8):

        def store(i, v, r=r):
            zs[i + 1, 8 + r : 16 + r, :] = v

        sections(lambda i, r=r: flat[i, r : r + 8, :], store, 0, 15, 8, 1, zend)
    for s in range(10):
        rows(zs, y1, s, 32, 1, yend)
        head, tail = route(y1[s], (0, 1, 5), 48)
        ea[0, s] = ea_in[0, s] + head
        eb[1, s] = eb_in[1, s] + tail
        ea[1, s] = ea_in[1, s]
        eb[0, s] = eb_in[0, s]
    for r in range(0, 48, 8):

        def store(i, v, r=r):
            z2[i + 1, r : r + 8, :] = v

        sections(lambda i, r=r: y1[i + 1, r : r + 8, :], store, -1, 8, 4, 2, zend)
    for s in range(7):
        rows(z2, y2, s, 16, 2, yend)
        head, tail = route(y2[s], (1, 2, 6), 32)
        f2[0, s] = f2_in[0, s] + head
        f2[1, s] = f2_in[1, s] + tail
    for r in range(0, 32, 8):

        def store(i, v, r=r):
            z3[i + 1, r : r + 8, :] = v

        sections(lambda i, r=r: y2[i + 1, r : r + 8, :], store, -1, 5, 2, 2, zend)
    for s in range(5):
        rows(z3, y3, s, 8, 2, yend)
        head, tail = route(y3[s], (3, 2, 7), 32)
        f3[0, s] = f3_in[0, s] + head + tail

    def emit(dst, high):
        for blk in range(4):
            e = ea if blk < 2 else eb
            for s in range(10):
                at = 40 if high else 7
                dst[blk * 10 + s : blk * 10 + s + 1, :] = e[blk % 2, s, at : at + 1, :]
        for j in range(2 if high else 1):
            for blk in range(2):
                for s in range(7):
                    at, to = 24 + j if high else 7, 40 + j * 14 + blk * 7 + s
                    dst[to : to + 1, :] = f2[blk, s, at : at + 1, :]
            for s in range(5):
                at, to = 16 + j if high else 7, 68 + j * 5 + s
                dst[to : to + 1, :] = f3[0, s, at : at + 1, :]

    odd_row = lax.rem(lax.axis_index("gy"), 2) == 1
    for dst, when in ((ya, odd_row), (yb, jnp.logical_not(odd_row))):
        pl.when(when)(lambda dst=dst: emit(dst, False))
        pl.when(jnp.logical_not(when))(lambda dst=dst: emit(dst, True))


def rows_kernel(pa, pb, ea_in, eb_in, f2_in, f3_in, ea, eb, f2, f3, za, zb):
    odd = lax.rem(lax.axis_index("gy"), 2) == 1
    ea[...], eb[...], f2[...], f3[...] = ea_in[...], eb_in[...], f2_in[...], f3_in[...]

    def got(at):
        a, b = pa[at : at + 1, :], pb[at : at + 1, :]
        return jnp.where(odd, a, b), jnp.where(odd, b, a)

    def add(ref, blk, s, at, v):
        ref[blk, s, at : at + 1, :] = ref[blk, s, at : at + 1, :] + v

    for blk in range(4):
        e = ea if blk < 2 else eb
        for s in range(10):
            under, over = got(blk * 10 + s)
            add(e, blk % 2, s, 8, under)
            add(e, blk % 2, s, 39, over)
    for j in range(2):
        for blk in range(2):
            for s in range(7):
                under, over = got(40 + j * 14 + blk * 7 + s)
                add(f2, blk, s, 8 + j, under)
                if j == 0:
                    add(f2, blk, s, 23, over)
        for s in range(5):
            under, over = got(68 + j * 5 + s)
            add(f3, 0, s, 8 + j, under)
            if j == 0:
                add(f3, 0, s, 15, over)

    def emit(dst, high):
        for blk in range(4):
            e = ea if blk < 2 else eb
            dst[blk * 32 : blk * 32 + 32, :] = e[blk % 2, 9 if high else 0, 8:40, :]
        for j in range(2 if high else 1):
            for blk in range(2):
                to = 128 + j * 32 + blk * 16
                dst[to : to + 16, :] = f2[blk, 5 + j if high else 0, 8:24, :]
            to = 192 + j * 8
            dst[to : to + 8, :] = f3[0, 3 + j if high else 0, 8:16, :]

    odd_slab = lax.rem(lax.axis_index("gz"), 2) == 1
    for dst, when in ((za, odd_slab), (zb, jnp.logical_not(odd_slab))):
        pl.when(when)(lambda dst=dst: emit(dst, False))
        pl.when(jnp.logical_not(when))(lambda dst=dst: emit(dst, True))


def sections_kernel(pa, pb, ea, eb, f2, f3, one, two, three):
    odd = lax.rem(lax.axis_index("gz"), 2) == 1

    def got(at, tall):
        a, b = pa[at : at + tall, :], pb[at : at + tall, :]
        return jnp.where(odd, a, b), jnp.where(odd, b, a)

    for blk in range(4):
        e = ea if blk < 2 else eb
        under, over = got(blk * 32, 32)
        for z in range(8):
            v = e[blk % 2, z + 1, 8:40, :]
            v = v + under if z == 0 else v + over if z == 7 else v
            one[z, :, blk * 128 : blk * 128 + 128] = v
    for blk in range(2):
        under, over = got(128 + blk * 16, 16)
        further, _ = got(160 + blk * 16, 16)
        for z in range(4):
            v = f2[blk, z + 1, 8:24, :]
            v = v + under if z == 0 else v + further if z == 1 else v + over if z == 3 else v
            two[z, :, blk * 128 : blk * 128 + 128] = v
    under, over = got(192, 8)
    further, _ = got(200, 8)
    three[0] = f3[0, 1, 8:16, :] + under
    three[1] = f3[0, 2, 8:16, :] + further + over


def shape(*dims):
    return jax.ShapeDtypeStruct(dims, f32)


def swap(x, axis, first):
    count = lax.axis_size(axis)
    pairs = []
    for i in range(first, count - 1, 2):
        pairs += [(i, i + 1), (i + 1, i)]
    return lax.ppermute(x, axis, pairs)


def call(kernel, outs, scratch, args, name, flops, moved, specs=None, aliases=None):
    return pl.pallas_call(
        kernel,
        out_shape=outs,
        in_specs=specs or [VMEM] * len(args),
        out_specs=[VMEM] * len(outs),
        scratch_shapes=scratch,
        input_output_aliases=aliases or {},
        cost_estimate=pl.CostEstimate(flops=flops, bytes_accessed=moved, transcendentals=0),
        name=name,
    )(*args)


def on_device(volume):
    w = jnp.asarray(column_weights(), bf16)
    we = jnp.asarray(edge_weights(), bf16)
    ws = jnp.asarray(shell_weights(), bf16)
    buf = pltpu.VMEM
    shells = pl.pallas_call(
        shell_kernel,
        grid=(1,),
        out_shape=shape(8, 1024),
        in_specs=[
            pl.BlockSpec((16, 64, 128), lambda i: (0, 0, 0)),
            pl.BlockSpec((16, 64, 128), lambda i: (0, 0, 7)),
            pl.BlockSpec((16, 256), lambda i: (0, 0)),
        ],
        out_specs=pl.BlockSpec((8, 1024), lambda i: (0, 0)),
        cost_estimate=pl.CostEstimate(flops=10**8, bytes_accessed=1 << 20, transcendentals=0),
        name="shells",
    )(volume, volume, ws)
    xa = swap(shells, "gx", 0)
    xb = swap(shells, "gx", 1)
    block = [buf((2, 10, 80, 128), f32), buf((2, 10, 48, 128), f32), buf((480, 768), bf16), buf((480, 256), f32)]
    e, f2s, f3s = shape(2, 10, 48, 128), shape(2, 7, 32, 128), shape(1, 5, 32, 128)
    ea, side = call(first_kernel, [e, shape(10, 48, 128)], block, (volume, w), "first", 4 * 10**9, 1 << 21)
    ea, eb, f2, f3 = call(
        second_kernel,
        [e, e, f2s, f3s],
        block
        + [buf((10, 48, 128), f32)]
        + [buf((5, 7, 48, 128), f32), buf((5, 7, 32, 128), f32), buf((448, 768), bf16), buf((224, 384), bf16)]
        + [buf((448, 256), f32), buf((224, 256), f32), buf((7, 32, 128), f32)]
        + [buf((3, 5, 32, 128), f32), buf((3, 5, 32, 128), f32), buf((160, 768), bf16), buf((160, 384), bf16)]
        + [buf((160, 256), f32), buf((160, 256), f32)],
        (volume, w, we, ea, side),
        "second",
        5 * 10**9,
        1 << 21,
    )
    keepers = {2: 0, 3: 1, 4: 2, 5: 3}
    ea, eb, f2, f3, ya, yb = call(
        columns_kernel,
        [e, e, f2s, f3s, shape(80, 128), shape(80, 128)],
        [buf((16, 64, 128), f32), buf((10, 80, 128), f32), buf((10, 48, 128), f32), buf((7, 48, 128), f32)]
        + [buf((7, 32, 128), f32), buf((5, 32, 128), f32), buf((5, 32, 128), f32)],
        (xa, xb, ea, eb, f2, f3),
        "columns",
        10**8,
        1 << 20,
    )
    ya, yb = swap(ya, "gy", 0), swap(yb, "gy", 1)
    ea, eb, f2, f3, za, zb = call(
        rows_kernel,
        [e, e, f2s, f3s, shape(208, 128), shape(208, 128)],
        [],
        (ya, yb, ea, eb, f2, f3),
        "rows",
        10**8,
        1 << 20,
    )
    za, zb = swap(za, "gz", 0), swap(zb, "gz", 1)
    return tuple(
        call(
            sections_kernel,
            [shape(8, 32, 512), shape(4, 16, 256), shape(2, 8, 128)],
            [],
            (za, zb, ea, eb, f2, f3),
            "sections",
            10**8,
            1 << 20,
        )
    )


def solution(mesh):
    spec = P("gz", "gy", "gx")
    return jax.shard_map(
        on_device, mesh=mesh, in_specs=(spec,), out_specs=(spec,) * 3, check_vma=False
    )
```

time: 222 us -> 48.5 us (0.22)
  the two profiles are of different devices: /device:TPU:66 before, /device:TPU:21 now
where the time goes in v1:
time: 48.5 us; the launch traced here: 48.2 us
  Pallas kernels  20.3 us (42%)
  starting transfers between devices  17.3 us (36%)
  waiting for transfers between devices  8.09 us (17%)
  local copies, waits for them, and re-layouts  1.86 us (4%)
  between operations  0.69 us (1%)
    pallas_call x5, Pallas kernels, call(): pl.pallas_call(kernel, out_shape=outs, in_specs=specs or [VMEM] * len(arg...  18 us
    ppermute x6, starting transfers between devices, swap(): return lax.ppermute(x, axis, pairs)  17.3 us
    ppermute x6, waiting for transfers between devices, swap(): return lax.ppermute(x, axis, pairs)  8.09 us
    pallas_call x1, Pallas kernels, on_device(): pl.pallas_call(shell_kernel, grid=(1,), out_shape=shape(8, 1024), in_spec...  2.36 us
    unnamed x12, local copies, waits for them, and re-layouts  1.86 us
  transfers between devices with their start and end apart: 6, of which 3 were waited for; matrix products, arithmetic and copies ran while one was open for 0% of the time, Pallas kernels for 21%

profile of v1, /device:TPU:21, one launch (start us, length us, event | category | flops | bytes accessed | tf_op | source)
XLA Modules:
  0.0 48.2 jit_solution(10789835531112429312)
XLA Ops:
  0.6 2.4 %shells.1 = f32[8,1024]{1,0:T(8,128)} custom-call(f32[16,64,1024]{2,1,0:T(8,128)} %volume.3, f32[16,64,1024]{2,1,0:T(8,128)} %volume.3, bf16[16,256]{1,0:T(8,128)(2,1)} %constant.8.clone.w), custom_call_target="tpu_custom_call" | custom-call | flops 100000000 | bytes 1048576 | tf_op jit(solution)/shard_map/shells/pallas_call | solution.py:433
  3.0 0.7 %collective-permute-start.1 = (f32[8,1024]{1,0:T(8,128)}, f32[8,1024]{1,0:T(8,128)S(1)}, u32[]{:S(2)}, u32[]{:S(2)}) collective-permute-start(f32[8,1024]{1,0:T(8,128)} %shells.1), channel_id=1, source_target_pairs={{64,128},{128,64},{65,129},{129,65},{66,130},{130,66},{67,131},{13... | collective-permute-start | bytes 98312 | tf_op jit(solution)/shard_map/ppermute | solution.py:412
  3.7 8.5 %collective-permute-start = (f32[8,1024]{1,0:T(8,128)}, f32[8,1024]{1,0:T(8,128)S(1)}, u32[]{:S(2)}, u32[]{:S(2)}) collective-permute-start(f32[8,1024]{1,0:T(8,128)} %shells.1), channel_id=1, source_target_pairs={{0,64},{64,0},{128,192},{192,128},{1,65},{65,1},{129,193},{193,129... | collective-permute-start | bytes 98312 | tf_op jit(solution)/shard_map/ppermute | solution.py:412
  12.2 4.5 %first.1 = (f32[2,10,48,128]{3,2,1,0:T(8,128)}, f32[10,48,128]{2,1,0:T(8,128)}) custom-call(f32[16,64,1024]{2,1,0:T(8,128)} %volume.3, bf16[768,256]{1,0:T(8,128)(2,1)} %constant.6.clone.w), custom_call_target="tpu_custom_call" | custom-call | flops 4000000000 | bytes 2097152 | tf_op jit(solution)/shard_map/first/pallas_call | solution.py:416
  16.6 5.8 %second.1 = (f32[2,10,48,128]{3,2,1,0:T(8,128)}, f32[2,10,48,128]{3,2,1,0:T(8,128)}, f32[2,7,32,128]{3,2,1,0:T(8,128)}, f32[1,5,32,128]{3,2,1,0:T(8,128)}) custom-call(f32[16,64,1024]{2,1,0:T(8,128)} %volume.3, bf16[768,256]{1,0:T(8,128)(2,1)} %constant.6.clone.w, bf16[384,256]{1,0:T(8,128)(2,1)} %constant.7.clone.we, ...), custom_call_target="tpu_custom_call" | custom-call | flops 5000000000 | bytes 2097152 | tf_op jit(solution)/shard_map/second/pallas_call | solution.py:416
  22.4 0.0 collective-permute-done.1.pb
  22.4 0.0 copy-start.4
  22.4 0.0 collective-permute-done.pa
  22.4 0.0 copy-start.5
  22.5 0.6 %copy-done.4 = f32[8,1024]{1,0:T(8,128)} copy-done((f32[8,1024]{1,0:T(8,128)}, f32[8,1024]{1,0:T(8,128)S(1)}, u32[]{:S(2)}) %copy-start.4) | copy-done | bytes 32792
  23.0 0.0 copy-done.5
  23.1 2.9 %columns.1 = (f32[2,10,48,128]{3,2,1,0:T(8,128)}, f32[2,10,48,128]{3,2,1,0:T(8,128)}, f32[2,7,32,128]{3,2,1,0:T(8,128)}, f32[1,5,32,128]{3,2,1,0:T(8,128)}, f32[80,128]{1,0:T(8,128)}, /*index=5*/f32[80,128]{1,0:T(8,128)}) custom-call(f32[8,1024]{1,0:T(8,128)} %copy-done.5, f32[8,1024]{1,0:T(8,128)} %copy-done.4, f32[2,10,48,128]{3,2,1,0:T(8,128)} %get-tuple-element.23.ea_in, ...), custom_call_target="tpu_custom_call" | custom-call | flops 100000000 | bytes 1048576 | tf_op jit(solution)/shard_map/columns/pallas_call | solution.py:416
  26.0 1.0 %collective-permute-start.2 = (f32[80,128]{1,0:T(8,128)}, f32[80,128]{1,0:T(8,128)S(1)}, u32[]{:S(2)}, u32[]{:S(2)}) collective-permute-start(f32[80,128]{1,0:T(8,128)} %get-tuple-element.27), channel_id=1, source_target_pairs={{0,16},{16,0},{32,48},{48,32},{1,17},{17,1},{33,49},{49,33},{2,18}... | collective-permute-start | bytes 122888 | tf_op jit(solution)/shard_map/ppermute | solution.py:412
  27.0 1.9 %collective-permute-start.3 = (f32[80,128]{1,0:T(8,128)}, f32[80,128]{1,0:T(8,128)S(1)}, u32[]{:S(2)}, u32[]{:S(2)}) collective-permute-start(f32[80,128]{1,0:T(8,128)} %get-tuple-element.28), channel_id=1, source_target_pairs={{16,32},{32,16},{17,33},{33,17},{18,34},{34,18},{19,35},{35,19},{2... | collective-permute-start | bytes 122888 | tf_op jit(solution)/shard_map/ppermute | solution.py:412
  28.9 0.2 collective-permute-done.2.pa
  29.0 0.0 copy-start.2
  29.0 2.9 %collective-permute-done.3.pb = f32[80,128]{1,0:T(8,128)S(1)} collective-permute-done((f32[80,128]{1,0:T(8,128)}, f32[80,128]{1,0:T(8,128)S(1)}, u32[]{:S(2)}, u32[]{:S(2)}) %collective-permute-start.3) | collective-permute-done | bytes 40992 | tf_op jit(solution)/shard_map/ppermute | solution.py:412
  31.9 0.0 copy-start.3
  31.9 0.0 copy-done.2
  31.9 0.6 %copy-done.3 = f32[80,128]{1,0:T(8,128)} copy-done((f32[80,128]{1,0:T(8,128)}, f32[80,128]{1,0:T(8,128)S(1)}, u32[]{:S(2)}) %copy-start.3) | copy-done | bytes 40984
  32.5 2.6 %rows.1 = (f32[2,10,48,128]{3,2,1,0:T(8,128)}, f32[2,10,48,128]{3,2,1,0:T(8,128)}, f32[2,7,32,128]{3,2,1,0:T(8,128)}, f32[1,5,32,128]{3,2,1,0:T(8,128)}, f32[208,128]{1,0:T(8,128)}, /*index=5*/f32[208,128]{1,0:T(8,128)}) custom-call(f32[80,128]{1,0:T(8,128)} %copy-done.2, f32[80,128]{1,0:T(8,128)} %copy-done.3, f32[2,10,48,128]{3,2,1,0:T(8,128)} %get-tuple-element.29.ea_in, ...), custom_call_target="tpu_custom_call" | custom-call | flops 100000000 | bytes 1048576 | tf_op jit(solution)/shard_map/rows/pallas_call | solution.py:416
  35.1 2.7 %collective-permute-start.4 = (f32[208,128]{1,0:T(8,128)}, f32[208,128]{1,0:T(8,128)S(1)}, u32[]{:S(2)}, u32[]{:S(2)}) collective-permute-start(f32[208,128]{1,0:T(8,128)} %get-tuple-element.33), channel_id=1, source_target_pairs={{0,1},{1,0},{2,3},{3,2},{4,5},{5,4},{6,7},{7,6},{8,9},{9,8},{10,11... | collective-permute-start | bytes 319496 | tf_op jit(solution)/shard_map/ppermute | solution.py:412
  37.8 2.5 %collective-permute-start.5 = (f32[208,128]{1,0:T(8,128)}, f32[208,128]{1,0:T(8,128)S(1)}, u32[]{:S(2)}, u32[]{:S(2)}) collective-permute-start(f32[208,128]{1,0:T(8,128)} %get-tuple-element.34), channel_id=1, source_target_pairs={{1,2},{2,1},{3,4},{4,3},{5,6},{6,5},{7,8},{8,7},{9,10},{10,9},{11,... | collective-permute-start | bytes 319496 | tf_op jit(solution)/shard_map/ppermute | solution.py:412
  40.3 0.0 collective-permute-done.4.pa
  40.3 0.0 copy-start
  40.3 5.1 %collective-permute-done.5.pb = f32[208,128]{1,0:T(8,128)S(1)} collective-permute-done((f32[208,128]{1,0:T(8,128)}, f32[208,128]{1,0:T(8,128)S(1)}, u32[]{:S(2)}, u32[]{:S(2)}) %collective-permute-start.5) | collective-permute-done | bytes 106528 | tf_op jit(solution)/shard_map/ppermute | solution.py:412
  45.4 0.0 copy-start.1
  45.4 0.0 copy-done
  45.4 0.6 %copy-done.1 = f32[208,128]{1,0:T(8,128)} copy-done((f32[208,128]{1,0:T(8,128)}, f32[208,128]{1,0:T(8,128)S(1)}, u32[]{:S(2)}) %copy-start.1) | copy-done | bytes 106520
  46.0 2.2 %sections.1 = (f32[8,32,512]{2,1,0:T(8,128)}, f32[4,16,256]{2,1,0:T(8,128)}, f32[2,8,128]{2,1,0:T(8,128)}) custom-call(f32[208,128]{1,0:T(8,128)} %copy-done, f32[208,128]{1,0:T(8,128)} %copy-done.1, f32[2,10,48,128]{3,2,1,0:T(8,128)} %get-tuple-element.35.ea, f32[2,10,48,128]{3,2,1,0:T(8,128)} %get-tuple-element.36.eb, ...), custom_call_target="tpu_custom_call" | custom-call | flops 100000000 | bytes 1048576 | tf_op jit(solution)/shard_map/sections/pallas_call | solution.py:416
Async XLA Ops:
  3.0 19.4 %collective-permute-start.1 = (f32[8,1024]{1,0:T(8,128)}, f32[8,1024]{1,0:T(8,128)S(1)}, u32[]{:S(2)}, u32[]{:S(2)}) collective-permute-start(f32[8,1024]{1,0:T(8,128)} %shells.1), channel_id=1, source_target_pairs={{64,128},{128,64},{65,129},{129,65},{66,130},{130,66},{67,131},{13... | collective-permute-start | bytes 98312 | tf_op jit(solution)/shard_map/ppermute | solution.py:412
  3.7 18.8 %collective-permute-start = (f32[8,1024]{1,0:T(8,128)}, f32[8,1024]{1,0:T(8,128)S(1)}, u32[]{:S(2)}, u32[]{:S(2)}) collective-permute-start(f32[8,1024]{1,0:T(8,128)} %shells.1), channel_id=1, source_target_pairs={{0,64},{64,0},{128,192},{192,128},{1,65},{65,1},{129,193},{193,129... | collective-permute-start | bytes 98312 | tf_op jit(solution)/shard_map/ppermute | solution.py:412
  22.4 0.6 %copy-start.4 = (f32[8,1024]{1,0:T(8,128)}, f32[8,1024]{1,0:T(8,128)S(1)}, u32[]{:S(2)}) copy-start(f32[8,1024]{1,0:T(8,128)S(1)} %collective-permute-done.1.pb) | copy-start | bytes 98308
  22.4 0.6 %copy-start.5 = (f32[8,1024]{1,0:T(8,128)}, f32[8,1024]{1,0:T(8,128)S(1)}, u32[]{:S(2)}) copy-start(f32[8,1024]{1,0:T(8,128)S(1)} %collective-permute-done.pa) | copy-start | bytes 98308
  26.0 3.1 %collective-permute-start.2 = (f32[80,128]{1,0:T(8,128)}, f32[80,128]{1,0:T(8,128)S(1)}, u32[]{:S(2)}, u32[]{:S(2)}) collective-permute-start(f32[80,128]{1,0:T(8,128)} %get-tuple-element.27), channel_id=1, source_target_pairs={{0,16},{16,0},{32,48},{48,32},{1,17},{17,1},{33,49},{49,33},{2,18}... | collective-permute-start | bytes 122888 | tf_op jit(solution)/shard_map/ppermute | solution.py:412
  27.0 4.9 %collective-permute-start.3 = (f32[80,128]{1,0:T(8,128)}, f32[80,128]{1,0:T(8,128)S(1)}, u32[]{:S(2)}, u32[]{:S(2)}) collective-permute-start(f32[80,128]{1,0:T(8,128)} %get-tuple-element.28), channel_id=1, source_target_pairs={{16,32},{32,16},{17,33},{33,17},{18,34},{34,18},{19,35},{35,19},{2... | collective-permute-start | bytes 122888 | tf_op jit(solution)/shard_map/ppermute | solution.py:412
  29.0 2.9 %copy-start.2 = (f32[80,128]{1,0:T(8,128)}, f32[80,128]{1,0:T(8,128)S(1)}, u32[]{:S(2)}) copy-start(f32[80,128]{1,0:T(8,128)S(1)} %collective-permute-done.2.pa) | copy-start | bytes 122884
  31.9 0.6 %copy-start.3 = (f32[80,128]{1,0:T(8,128)}, f32[80,128]{1,0:T(8,128)S(1)}, u32[]{:S(2)}) copy-start(f32[80,128]{1,0:T(8,128)S(1)} %collective-permute-done.3.pb) | copy-start | bytes 122884
  35.1 5.2 %collective-permute-start.4 = (f32[208,128]{1,0:T(8,128)}, f32[208,128]{1,0:T(8,128)S(1)}, u32[]{:S(2)}, u32[]{:S(2)}) collective-permute-start(f32[208,128]{1,0:T(8,128)} %get-tuple-element.33), channel_id=1, source_target_pairs={{0,1},{1,0},{2,3},{3,2},{4,5},{5,4},{6,7},{7,6},{8,9},{9,8},{10,11... | collective-permute-start | bytes 319496 | tf_op jit(solution)/shard_map/ppermute | solution.py:412
  37.8 7.6 %collective-permute-start.5 = (f32[208,128]{1,0:T(8,128)}, f32[208,128]{1,0:T(8,128)S(1)}, u32[]{:S(2)}, u32[]{:S(2)}) collective-permute-start(f32[208,128]{1,0:T(8,128)} %get-tuple-element.34), channel_id=1, source_target_pairs={{1,2},{2,1},{3,4},{4,3},{5,6},{6,5},{7,8},{8,7},{9,10},{10,9},{11,... | collective-permute-start | bytes 319496 | tf_op jit(solution)/shard_map/ppermute | solution.py:412
  40.3 5.1 %copy-start = (f32[208,128]{1,0:T(8,128)}, f32[208,128]{1,0:T(8,128)S(1)}, u32[]{:S(2)}) copy-start(f32[208,128]{1,0:T(8,128)S(1)} %collective-permute-done.4.pa) | copy-start | bytes 319492
  45.4 0.6 %copy-start.1 = (f32[208,128]{1,0:T(8,128)}, f32[208,128]{1,0:T(8,128)S(1)}, u32[]{:S(2)}) copy-start(f32[208,128]{1,0:T(8,128)S(1)} %collective-permute-done.5.pb) | copy-start | bytes 319492

commit v2 on v1

--- a/solution.py
+++ b/solution.py
@@ -164,7 +164,8 @@
     res[...] = matmul(ops[...], w[...])
 
 
-def first_kernel(volume, w, ea, side, zs, ys, ops, res):
+def first_kernel(volume, w, shells, ea, side, again, zs, ys, ops, res):
+    again[...] = shells[...]
     zend, yend = keep("gz", lax.axis_size("gz")), keep("gy", lax.axis_size("gy"))
     low = low_lanes(48)
     for b in range(2):
@@ -228,7 +229,6 @@
                   z3, y3, ops3, opse3, res3, rese3):
     zend, yend, xend = (keep(a, lax.axis_size(a)) for a in ("gz", "gy", "gx"))
     low = low_lanes(48)
-    ea[0] = ea_in[0]
     for b in range(2):
         level_one_block(volume, 2 + b, zs, ys, ops, res, w, zend, yend)
         for s in range(10):
@@ -236,7 +236,7 @@
             beside = res[s * 48 : s * 48 + 48, 128:]
             if b == 0:
                 eb[0, s] = main + jnp.where(low, side[s], 0.0)
-                ea[1, s] = ea_in[1, s] + jnp.where(low, 0.0, beside)
+                ea[1, s] = ea[1, s] + jnp.where(low, 0.0, beside)
                 h1[s] = beside
             else:
                 eb[1, s] = main + jnp.where(low, h1[s], 0.0)
@@ -279,10 +279,8 @@
     for s in range(10):
         rows(zs, y1, s, 32, 1, yend)
         head, tail = route(y1[s], (0, 1, 5), 48)
-        ea[0, s] = ea_in[0, s] + head
-        eb[1, s] = eb_in[1, s] + tail
-        ea[1, s] = ea_in[1, s]
-        eb[0, s] = eb_in[0, s]
+        ea[0, s] = ea[0, s] + head
+        eb[1, s] = eb[1, s] + tail
     for r in range(0, 48, 8):
 
         def store(i, v, r=r):
@@ -292,8 +290,8 @@
     for s in range(7):
         rows(z2, y2, s, 16, 2, yend)
         head, tail = route(y2[s], (1, 2, 6), 32)
-        f2[0, s] = f2_in[0, s] + head
-        f2[1, s] = f2_in[1, s] + tail
+        f2[0, s] = f2[0, s] + head
+        f2[1, s] = f2[1, s] + tail
     for r in range(0, 32, 8):
 
         def store(i, v, r=r):
@@ -303,7 +301,7 @@
     for s in range(5):
         rows(z3, y3, s, 8, 2, yend)
         head, tail = route(y3[s], (3, 2, 7), 32)
-        f3[0, s] = f3_in[0, s] + head + tail
+        f3[0, s] = f3[0, s] + head + tail
 
     def emit(dst, high):
         for blk in range(4):
@@ -328,8 +326,6 @@
 
 def rows_kernel(pa, pb, ea_in, eb_in, f2_in, f3_in, ea, eb, f2, f3, za, zb):
     odd = lax.rem(lax.axis_index("gy"), 2) == 1
-    ea[...], eb[...], f2[...], f3[...] = ea_in[...], eb_in[...], f2_in[...], f3_in[...]
-
     def got(at):
         a, b = pa[at : at + 1, :], pb[at : at + 1, :]
         return jnp.where(odd, a, b), jnp.where(odd, b, a)
@@ -412,7 +408,7 @@
     return lax.ppermute(x, axis, pairs)
 
 
-def call(kernel, outs, scratch, args, name, flops, moved, specs=None, aliases=None):
+def call(kernel, outs, scratch, args, name, flops, moved, specs=None, aliases=None, limit=16):
     return pl.pallas_call(
         kernel,
         out_shape=outs,
@@ -420,6 +416,7 @@
         out_specs=[VMEM] * len(outs),
         scratch_shapes=scratch,
         input_output_aliases=aliases or {},
+        compiler_params=pltpu.CompilerParams(vmem_limit_bytes=limit << 20),
         cost_estimate=pl.CostEstimate(flops=flops, bytes_accessed=moved, transcendentals=0),
         name=name,
     )(*args)
@@ -440,14 +437,23 @@
             pl.BlockSpec((16, 256), lambda i: (0, 0)),
         ],
         out_specs=pl.BlockSpec((8, 1024), lambda i: (0, 0)),
+        compiler_params=pltpu.CompilerParams(vmem_limit_bytes=8 << 20),
         cost_estimate=pl.CostEstimate(flops=10**8, bytes_accessed=1 << 20, transcendentals=0),
         name="shells",
     )(volume, volume, ws)
     xa = swap(shells, "gx", 0)
-    xb = swap(shells, "gx", 1)
     block = [buf((2, 10, 80, 128), f32), buf((2, 10, 48, 128), f32), buf((480, 768), bf16), buf((480, 256), f32)]
     e, f2s, f3s = shape(2, 10, 48, 128), shape(2, 7, 32, 128), shape(1, 5, 32, 128)
-    ea, side = call(first_kernel, [e, shape(10, 48, 128)], block, (volume, w), "first", 4 * 10**9, 1 << 21)
+    ea, side, again = call(
+        first_kernel,
+        [e, shape(10, 48, 128), shape(8, 1024)],
+        block,
+        (volume, w, shells),
+        "first",
+        4 * 10**9,
+        1 << 21,
+    )
+    xb = swap(again, "gx", 1)
     ea, eb, f2, f3 = call(
         second_kernel,
         [e, e, f2s, f3s],
@@ -461,6 +467,7 @@
         "second",
         5 * 10**9,
         1 << 21,
+        aliases={3: 0},
     )
     keepers = {2: 0, 3: 1, 4: 2, 5: 3}
     ea, eb, f2, f3, ya, yb = call(
@@ -472,6 +479,7 @@
         "columns",
         10**8,
         1 << 20,
+        aliases=keepers,
     )
     ya, yb = swap(ya, "gy", 0), swap(yb, "gy", 1)
     ea, eb, f2, f3, za, zb = call(
@@ -482,6 +490,7 @@
         "rows",
         10**8,
         1 << 20,
+        aliases=keepers,
     )
     za, zb = swap(za, "gz", 0), swap(zb, "gz", 1)
     return tuple(

time: 48.5 us -> 33.4 us (0.69)
  the two profiles are of different devices: /device:TPU:21 before, /device:TPU:85 now
where the time goes in v2:
time: 33.4 us; the launch traced here: 33.2 us
  starting transfers between devices  14.2 us (43%)
  waiting for transfers between devices  7.67 us (23%)
  Pallas kernels  6.05 us (18%)
  local copies, waits for them, and re-layouts  4.56 us (14%)
  between operations  0.75 us (2%)
    ppermute x6, starting transfers between devices, swap(): return lax.ppermute(x, axis, pairs)  14.2 us
    ppermute x6, waiting for transfers between devices, swap(): return lax.ppermute(x, axis, pairs)  7.67 us
    pallas_call x5, Pallas kernels, call(): pl.pallas_call(kernel, out_shape=outs, in_specs=specs or [VMEM] * len(arg...  5.54 us
    unnamed x10, local copies, waits for them, and re-layouts  4.56 us
  transfers between devices with their start and end apart: 6, of which 2 were waited for; matrix products, arithmetic and copies ran while one was open for 0% of the time, Pallas kernels for 12%

profile of v2, /device:TPU:85, one launch (start us, length us, event | category | flops | bytes accessed | tf_op | source)
XLA Modules:
  0.0 33.2 jit_solution(17857217578815188577)
XLA Ops:
  0.6 0.0 copy-start
  0.6 2.2 %copy-done = f32[16,64,1024]{2,1,0:T(8,128)S(1)} copy-done((f32[16,64,1024]{2,1,0:T(8,128)S(1)}, f32[16,64,1024]{2,1,0:T(8,128)}, u32[]{:S(2)}) %copy-start) | copy-done | bytes 4194328
  2.8 0.0 copy-start.2
  2.8 0.7 %copy-done.2 = bf16[16,256]{1,0:T(8,128)(2,1)S(1)} copy-done((bf16[16,256]{1,0:T(8,128)(2,1)S(1)}, bf16[16,256]{1,0:T(8,128)(2,1)}, u32[]{:S(2)}) %copy-start.2) | copy-done | bytes 8216
  3.5 0.0 copy-start.1
  3.5 0.0 copy-start.3
  3.5 0.5 %shells.1 = f32[8,1024]{1,0:T(8,128)S(1)} custom-call(f32[16,64,1024]{2,1,0:T(8,128)S(1)} %copy-done, f32[16,64,1024]{2,1,0:T(8,128)S(1)} %copy-done, bf16[16,256]{1,0:T(8,128)(2,1)S(1)} %copy-done.2), custom_call_target="tpu_custom_call" | custom-call | flops 100000000 | bytes 1048576 | tf_op jit(solution)/shard_map/shells/pallas_call | solution.py:430
  4.0 0.0 copy-start.4
  4.0 0.1 collective-permute-start
  4.1 1.6 %copy-done.1 = f32[16,64,1024]{2,1,0:T(8,128)S(1)} copy-done((f32[16,64,1024]{2,1,0:T(8,128)S(1)}, f32[16,64,1024]{2,1,0:T(8,128)}, u32[]{:S(2)}) %copy-start.1) | copy-done | bytes 4194328
  5.7 0.1 copy-done.3
  5.8 1.4 %first.1 = (f32[2,10,48,128]{3,2,1,0:T(8,128)S(1)}, f32[10,48,128]{2,1,0:T(8,128)S(1)}, f32[8,1024]{1,0:T(8,128)S(1)}) custom-call(f32[16,64,1024]{2,1,0:T(8,128)S(1)} %copy-done.1, bf16[768,256]{1,0:T(8,128)(2,1)S(1)} %copy-done.3, f32[8,1024]{1,0:T(8,128)S(1)} %shells.1), custom_call_target="tpu_custom_call" | custom-call | flops 4000000000 | bytes 2097152 | tf_op jit(solution)/shard_map/first/pallas_call | solution.py:412
  7.1 6.1 %collective-permute-start.1 = (f32[8,1024]{1,0:T(8,128)S(1)}, f32[8,1024]{1,0:T(8,128)S(1)}, u32[]{:S(2)}, u32[]{:S(2)}) collective-permute-start(f32[8,1024]{1,0:T(8,128)S(1)} %get-tuple-element.22), channel_id=1, source_target_pairs={{64,128},{128,64},{65,129},{129,65},{66,130},{130,66},{67,131},{13... | collective-permute-start | bytes 98312 | tf_op jit(solution)/shard_map/ppermute | solution.py:408
  13.3 0.0 copy-done.4
  13.3 2.6 %second.1 = (f32[2,10,48,128]{3,2,1,0:T(8,128)S(1)}, f32[2,10,48,128]{3,2,1,0:T(8,128)S(1)}, f32[2,7,32,128]{3,2,1,0:T(8,128)S(1)}, f32[1,5,32,128]{3,2,1,0:T(8,128)S(1)}) custom-call(f32[16,64,1024]{2,1,0:T(8,128)S(1)} %copy-done.1, bf16[768,256]{1,0:T(8,128)(2,1)S(1)} %copy-done.3, ...), custom_call_target="tpu_custom_call", output_to_operand_aliasing={{0}: (3, {})} | custom-call | flops 5000000000 | bytes 2097152 | tf_op jit(solution)/shard_map/second/pallas_call | solution.py:412
  15.9 0.0 collective-permute-done.pa
  15.9 0.0 collective-permute-done.1.pb
  15.9 0.5 %columns.1 = (f32[2,10,48,128]{3,2,1,0:T(8,128)S(1)}, f32[2,10,48,128]{3,2,1,0:T(8,128)S(1)}, f32[2,7,32,128]{3,2,1,0:T(8,128)S(1)}, f32[1,5,32,128]{3,2,1,0:T(8...) custom-call(f32[8,1024]{1,0:T(8,128)S(1)} %collective-permute-done.p, ...), custom_call_target="tpu_custom_call", output_to_operand_aliasing={{0}: (2, {}), {1}: (3, {}), {2}: (4, {}), {3}: (5, {})} | custom-call | flops 100000000 | bytes 1048576 | tf_op jit(solution)/shard_map/columns/pallas_call | solution.py:412
  16.5 1.1 %collective-permute-start.2 = (f32[80,128]{1,0:T(8,128)S(1)}, f32[80,128]{1,0:T(8,128)S(1)}, u32[]{:S(2)}, u32[]{:S(2)}) collective-permute-start(f32[80,128]{1,0:T(8,128)S(1)} %get-tuple-element.29), channel_id=1, source_target_pairs={{0,16},{16,0},{32,48},{48,32},{1,17},{17,1},{33,49},{49,33},{2,18}... | collective-permute-start | bytes 122888 | tf_op jit(solution)/shard_map/ppermute | solution.py:408
  17.6 1.9 %collective-permute-start.3 = (f32[80,128]{1,0:T(8,128)S(1)}, f32[80,128]{1,0:T(8,128)S(1)}, u32[]{:S(2)}, u32[]{:S(2)}) collective-permute-start(f32[80,128]{1,0:T(8,128)S(1)} %get-tuple-element.30), channel_id=1, source_target_pairs={{16,32},{32,16},{17,33},{33,17},{18,34},{34,18},{19,35},{35,19},{2... | collective-permute-start | bytes 122888 | tf_op jit(solution)/shard_map/ppermute | solution.py:408
  19.5 0.0 collective-permute-done.2.pa
  19.5 2.8 %collective-permute-done.3.pb = f32[80,128]{1,0:T(8,128)S(1)} collective-permute-done((f32[80,128]{1,0:T(8,128)S(1)}, f32[80,128]{1,0:T(8,128)S(1)}, u32[]{:S(2)}, u32[]{:S(2)}) %collective-permute-start.3) | collective-permute-done | bytes 40992 | tf_op jit(solution)/shard_map/ppermute | solution.py:408
  22.3 0.1 rows.1
  22.4 2.5 %collective-permute-start.4 = (f32[208,128]{1,0:T(8,128)S(1)}, f32[208,128]{1,0:T(8,128)S(1)}, u32[]{:S(2)}, u32[]{:S(2)}) collective-permute-start(f32[208,128]{1,0:T(8,128)S(1)} %get-tuple-element.35), channel_id=1, source_target_pairs={{0,1},{1,0},{2,3},{3,2},{4,5},{5,4},{6,7},{7,6},{8,9},{9,8},{10,11... | collective-permute-start | bytes 319496 | tf_op jit(solution)/shard_map/ppermute | solution.py:408
  24.9 2.5 %collective-permute-start.5 = (f32[208,128]{1,0:T(8,128)S(1)}, f32[208,128]{1,0:T(8,128)S(1)}, u32[]{:S(2)}, u32[]{:S(2)}) collective-permute-start(f32[208,128]{1,0:T(8,128)S(1)} %get-tuple-element.36), channel_id=1, source_target_pairs={{1,2},{2,1},{3,4},{4,3},{5,6},{6,5},{7,8},{8,7},{9,10},{10,9},{11,... | collective-permute-start | bytes 319496 | tf_op jit(solution)/shard_map/ppermute | solution.py:408
  27.4 0.0 collective-permute-done.4.pa
  27.4 4.9 %collective-permute-done.5.pb = f32[208,128]{1,0:T(8,128)S(1)} collective-permute-done((f32[208,128]{1,0:T(8,128)S(1)}, f32[208,128]{1,0:T(8,128)S(1)}, u32[]{:S(2)}, u32[]{:S(2)}) %collective-permute-start.5) | collective-permute-done | bytes 106528 | tf_op jit(solution)/shard_map/ppermute | solution.py:408
  32.3 0.9 %sections.1 = (f32[8,32,512]{2,1,0:T(8,128)}, f32[4,16,256]{2,1,0:T(8,128)}, f32[2,8,128]{2,1,0:T(8,128)}) custom-call(f32[208,128]{1,0:T(8,128)S(1)} %collective-permute-done.4.pa, f32[208,128]{1,0:T(8,128)S(1)} %collective-permute-done.5.pb, f32[2,10,48,128]{3,2,1,0:T(8,128)S(1)} %get-tuple-element.37.ea, f32[2,10,48,128]{3,2,1,0:T(8,128)S(1)} %get-tuple-element.38.eb, ...), custom_call_target="tpu_custom_call" | custom-call | flops 100000000 | bytes 1048576 | tf_op jit(solution)/shard_map/sections/pallas_call | solution.py:412
Async XLA Ops:
  0.6 2.2 %copy-start = (f32[16,64,1024]{2,1,0:T(8,128)S(1)}, f32[16,64,1024]{2,1,0:T(8,128)}, u32[]{:S(2)}) copy-start(f32[16,64,1024]{2,1,0:T(8,128)} %volume.3) | copy-start | bytes 12582916
  2.8 0.7 %copy-start.2 = (bf16[16,256]{1,0:T(8,128)(2,1)S(1)}, bf16[16,256]{1,0:T(8,128)(2,1)}, u32[]{:S(2)}) copy-start(bf16[16,256]{1,0:T(8,128)(2,1)} %constant.8.clone.w) | copy-start | bytes 24580
  3.5 2.2 %copy-start.1 = (f32[16,64,1024]{2,1,0:T(8,128)S(1)}, f32[16,64,1024]{2,1,0:T(8,128)}, u32[]{:S(2)}) copy-start(f32[16,64,1024]{2,1,0:T(8,128)} %volume.3) | copy-start | bytes 12582916
  3.5 2.3 %copy-start.3 = (bf16[768,256]{1,0:T(8,128)(2,1)S(1)}, bf16[768,256]{1,0:T(8,128)(2,1)}, u32[]{:S(2)}) copy-start(bf16[768,256]{1,0:T(8,128)(2,1)} %constant.6.clone.w) | copy-start | bytes 1179652
  4.0 9.2 %copy-start.4 = (bf16[384,256]{1,0:T(8,128)(2,1)S(1)}, bf16[384,256]{1,0:T(8,128)(2,1)}, u32[]{:S(2)}) copy-start(bf16[384,256]{1,0:T(8,128)(2,1)} %constant.7.clone.we) | copy-start | bytes 589828
  4.0 11.9 %collective-permute-start = (f32[8,1024]{1,0:T(8,128)S(1)}, f32[8,1024]{1,0:T(8,128)S(1)}, u32[]{:S(2)}, u32[]{:S(2)}) collective-permute-start(f32[8,1024]{1,0:T(8,128)S(1)} %shells.1), channel_id=1, source_target_pairs={{0,64},{64,0},{128,192},{192,128},{1,65},{65,1},{129,193},{193,129... | collective-permute-start | bytes 98312 | tf_op jit(solution)/shard_map/ppermute | solution.py:408
  7.1 8.8 %collective-permute-start.1 = (f32[8,1024]{1,0:T(8,128)S(1)}, f32[8,1024]{1,0:T(8,128)S(1)}, u32[]{:S(2)}, u32[]{:S(2)}) collective-permute-start(f32[8,1024]{1,0:T(8,128)S(1)} %get-tuple-element.22), channel_id=1, source_target_pairs={{64,128},{128,64},{65,129},{129,65},{66,130},{130,66},{67,131},{13... | collective-permute-start | bytes 98312 | tf_op jit(solution)/shard_map/ppermute | solution.py:408
  16.5 3.0 %collective-permute-start.2 = (f32[80,128]{1,0:T(8,128)S(1)}, f32[80,128]{1,0:T(8,128)S(1)}, u32[]{:S(2)}, u32[]{:S(2)}) collective-permute-start(f32[80,128]{1,0:T(8,128)S(1)} %get-tuple-element.29), channel_id=1, source_target_pairs={{0,16},{16,0},{32,48},{48,32},{1,17},{17,1},{33,49},{49,33},{2,18}... | collective-permute-start | bytes 122888 | tf_op jit(solution)/shard_map/ppermute | solution.py:408
  17.6 4.7 %collective-permute-start.3 = (f32[80,128]{1,0:T(8,128)S(1)}, f32[80,128]{1,0:T(8,128)S(1)}, u32[]{:S(2)}, u32[]{:S(2)}) collective-permute-start(f32[80,128]{1,0:T(8,128)S(1)} %get-tuple-element.30), channel_id=1, source_target_pairs={{16,32},{32,16},{17,33},{33,17},{18,34},{34,18},{19,35},{35,19},{2... | collective-permute-start | bytes 122888 | tf_op jit(solution)/shard_map/ppermute | solution.py:408
  22.4 5.0 %collective-permute-start.4 = (f32[208,128]{1,0:T(8,128)S(1)}, f32[208,128]{1,0:T(8,128)S(1)}, u32[]{:S(2)}, u32[]{:S(2)}) collective-permute-start(f32[208,128]{1,0:T(8,128)S(1)} %get-tuple-element.35), channel_id=1, source_target_pairs={{0,1},{1,0},{2,3},{3,2},{4,5},{5,4},{6,7},{7,6},{8,9},{9,8},{10,11... | collective-permute-start | bytes 319496 | tf_op jit(solution)/shard_map/ppermute | solution.py:408
  24.9 7.4 %collective-permute-start.5 = (f32[208,128]{1,0:T(8,128)S(1)}, f32[208,128]{1,0:T(8,128)S(1)}, u32[]{:S(2)}, u32[]{:S(2)}) collective-permute-start(f32[208,128]{1,0:T(8,128)S(1)} %get-tuple-element.36), channel_id=1, source_target_pairs={{1,2},{2,1},{3,4},{4,3},{5,6},{6,5},{7,8},{8,7},{9,10},{10,9},{11,... | collective-permute-start | bytes 319496 | tf_op jit(solution)/shard_map/ppermute | solution.py:408

commit v3 on v2

--- a/solution.py
+++ b/solution.py
@@ -48,20 +48,19 @@
     return h
 
 
-def shell_weights():
-    rows = [(1, 0), (2, 0), (2, 1), (3, 0), (3, 1), (1, -1), (2, -1), (3, -1)]
-    w = np.zeros((8, 256), np.float64)
-    for r, (level, place) in enumerate(rows):
+def shell_weights(first, tall):
+    lanes = [(1, 0), (1, -1), (2, 0), (2, 1), (2, -1), (3, 0), (3, 1), (3, -1)]
+    c = first + lax.broadcasted_iota(jnp.int32, (tall, 128), 0)
+    at = lax.broadcasted_iota(jnp.int32, (tall, 128), 1)
+    w = jnp.zeros((tall, 128), f32)
+    for r, (level, place) in enumerate(lanes):
         h = composite(level)
-        reach = len(h) // 2
+        start = place * 2**level - len(h) // 2 + (256 if place >= 0 else 0)
         for t in range(len(h)):
-            c = place * 2**level + t - reach
-            if r < 5 and -128 <= c < 0:
-                w[r, 256 + c] = h[t]
-            if r >= 5 and 0 <= c < 128:
-                w[r, c] = h[t]
-    high = w.astype(jnp.bfloat16).astype(np.float64)
-    return np.concatenate([high, w - high], axis=0).astype(np.float32)
+            if first <= start + t < first + tall and (start + t < 256 if place >= 0 else start + t >= 0):
+                w = jnp.where((at == r) & (c == start + t), float(h[t]), w)
+    high = w.astype(bf16)
+    return high, (w - high.astype(f32)).astype(bf16)
 
 
 def split(x):
@@ -136,13 +135,77 @@
     return jnp.dot(x, w, preferred_element_type=f32)
 
 
-def shell_kernel(left, right, w, out):
-    x = jnp.concatenate([left[...].reshape(1024, 128), right[...].reshape(1024, 128)], axis=1)
-    total = None
-    for piece in split(x):
-        t = lax.dot_general(w[...], piece, (((1,), (1,)), ((), ())), preferred_element_type=f32)
-        total = t if total is None else total + t
-    out[...] = total[:8] + total[8:]
+def pyramid(src, zs, flat, zend, yend):
+    z1, z2, z3 = zs
+    y1, y2, y3 = (flat.at[pl.ds(o, n * t)].reshape(n, t, 128) for o, n, t in TALL)
+    for s in range(10):
+        z1[s, 0:8, :] = jnp.zeros((8, 128), f32)
+        z1[s, 72:80, :] = jnp.zeros((8, 128), f32)
+    for r in range(0, 64, 8):
+
+        def store(i, v, r=r):
+            z1[i + 1, 8 + r : 16 + r, :] = v
+
+        sections(lambda i, r=r: src[i, r : r + 8, :], store, 0, 15, 8, 1, zend)
+    for s in range(10):
+        rows(z1, y1, s, 32, 1, yend)
+    for a, zb, b, used, first, half_z, half_y in (
+        (y1, z2, y2, 48, 8, 4, 16),
+        (y2, z3, y3, 32, 5, 2, 8),
+    ):
+        for r in range(0, used, 8):
+
+            def store(i, v, r=r, zb=zb):
+                zb[i + 1, r : r + 8, :] = v
+
+            sections(lambda i, r=r, a=a: a[i + 1, r : r + 8, :], store, -1, first, half_z, 2, zend)
+        for s in range(half_z + 3):
+            rows(zb, b, s, half_y, 2, yend)
+
+
+TALL = ((0, 10, 48), (480, 7, 32), (704, 5, 32))
+MIXED = ((3, 96), (5, 64))
+
+
+def shell_kernel(volume, out, kept, own, w, lines, prod, z1, z2, z3, flat, sems):
+    copies = []
+    for j, (first, wide) in enumerate(((0, 128), (896, 128), (128, 768))):
+        cols = pl.ds(first, wide)
+        copies.append(pltpu.make_async_copy(volume.at[:, :, cols], kept.at[:, :, cols], sems.at[j]))
+    for c in copies:
+        c.start()
+    zend, yend = keep("gz", lax.axis_size("gz")), keep("gy", lax.axis_size("gy"))
+    w[...] = jnp.zeros((768, 256), bf16)
+    for first in (0, 240):
+        for j, part in enumerate(shell_weights(first, 16)):
+            for q in range(3):
+                w[q * 256 + first : q * 256 + first + 16, j * 128 : j * 128 + 128] = part
+    for s in range(5):
+        flat[704 + s * 32 + 24 : 704 + s * 32 + 32, :] = jnp.zeros((8, 128), f32)
+    flat[864:896, :] = jnp.zeros((32, 128), f32)
+    out[16:24, :] = jnp.zeros((8, 128), f32)
+    copies[0].wait()
+    copies[1].wait()
+    for s in range(16):
+        pack([kept[s, :, 0:128], kept[s, :, 896:1024]], lines, s * 64)
+    prod[...] = matmul(lines[...], w[...])
+    for s in range(16):
+        lines_s = prod[s * 64 : s * 64 + 64, :]
+        own[s] = lines_s[:, :128] + lines_s[:, 128:]
+    pyramid(own, (z1, z2, z3), flat, zend, yend)
+    at = lax.broadcasted_iota(jnp.int32, (1, 128), 1)
+    mixed = dict(MIXED)
+    for j in range(7):
+        t = flat[j * 128 : j * 128 + 128, :].T
+        pick = [(t[0:1], None, t[1:2]), (t[2:3], t[3:4], t[4:5]), (t[5:6], t[6:7], t[7:8])]
+        level = 0 if j < 4 else 1 if j < 6 else 2
+        for q in range(3):
+            row = pick[level][q]
+            row = jnp.zeros((1, 128), f32) if row is None else row
+            if j in mixed:
+                row = jnp.where(at < mixed[j], row, pick[level + 1][q])
+            out[3 * j + q : 3 * j + q + 1, :] = row
+    copies[2].wait()
 
 
 def level_one_block(volume, at, zs, ys, ops, res, w, zend, yend):
@@ -248,60 +311,25 @@
                w, we, f3, None, 7, 2, 8, 32, 32, 32, zend, yend, xend)
 
 
-def route(x, base, tall):
-    at = lax.broadcasted_iota(jnp.int32, (tall, 128), 1)
-    first, count, last = base
-    head = x if first == 0 else pltpu.roll(x, 128 - first, axis=1)
-    tail = pltpu.roll(x, 127 - last, axis=1)
-    return jnp.where(at < count, head, 0.0), jnp.where(at == 127, tail, 0.0)
-
-
-def columns_kernel(pa, pb, ea_in, eb_in, f2_in, f3_in, ea, eb, f2, f3, ya, yb,
-                   flat, zs, y1, z2, y2, z3, y3):
-    zend, yend = keep("gz", lax.axis_size("gz")), keep("gy", lax.axis_size("gy"))
+def columns_kernel(pa, pb, ea_in, eb_in, f2_in, f3_in, ea, eb, f2, f3, ya, yb, flat):
     odd = lax.rem(lax.axis_index("gx"), 2) == 1
-    row = lax.broadcasted_iota(jnp.int32, (8, 128), 0)
-    for j in range(8):
-        a, b = pa[:, j * 128 : j * 128 + 128], pb[:, j * 128 : j * 128 + 128]
+    for j in range(7):
+        a, b = pa[3 * j : 3 * j + 3, :], pb[3 * j : 3 * j + 3, :]
         under, over = jnp.where(odd, a, b), jnp.where(odd, b, a)
-        mine = jnp.where(row < 5, under, over)
-        full = jnp.concatenate([mine, jnp.zeros((120, 128), f32)], axis=0)
-        flat[2 * j : 2 * j + 2] = full.T.reshape(2, 64, 128)
+        full = jnp.concatenate([under[:2], jnp.zeros((125, 128), f32), over[2:]], axis=0)
+        flat[j * 128 : j * 128 + 128, :] = full.T
+    low = low_lanes(48)
     for s in range(10):
-        zs[s, 0:8, :] = jnp.zeros((8, 128), f32)
-        zs[s, 72:80, :] = jnp.zeros((8, 128), f32)
-    for r in range(0, 64, 8):
-
-        def store(i, v, r=r):
-            zs[i + 1, 8 + r : 16 + r, :] = v
-
-        sections(lambda i, r=r: flat[i, r : r + 8, :], store, 0, 15, 8, 1, zend)
-    for s in range(10):
-        rows(zs, y1, s, 32, 1, yend)
-        head, tail = route(y1[s], (0, 1, 5), 48)
-        ea[0, s] = ea[0, s] + head
-        eb[1, s] = eb[1, s] + tail
-    for r in range(0, 48, 8):
-
-        def store(i, v, r=r):
-            z2[i + 1, r : r + 8, :] = v
-
-        sections(lambda i, r=r: y1[i + 1, r : r + 8, :], store, -1, 8, 4, 2, zend)
+        v = flat[s * 48 : s * 48 + 48, :]
+        ea[0, s] = ea[0, s] + jnp.where(low, v, 0.0)
+        eb[1, s] = eb[1, s] + jnp.where(low, 0.0, v)
+    low = low_lanes(32)
     for s in range(7):
-        rows(z2, y2, s, 16, 2, yend)
-        head, tail = route(y2[s], (1, 2, 6), 32)
-        f2[0, s] = f2[0, s] + head
-        f2[1, s] = f2[1, s] + tail
-    for r in range(0, 32, 8):
-
-        def store(i, v, r=r):
-            z3[i + 1, r : r + 8, :] = v
-
-        sections(lambda i, r=r: y2[i + 1, r : r + 8, :], store, -1, 5, 2, 2, zend)
+        v = flat[480 + s * 32 : 512 + s * 32, :]
+        f2[0, s] = f2[0, s] + jnp.where(low, v, 0.0)
+        f2[1, s] = f2[1, s] + jnp.where(low, 0.0, v)
     for s in range(5):
-        rows(z3, y3, s, 8, 2, yend)
-        head, tail = route(y3[s], (3, 2, 7), 32)
-        f3[0, s] = f3[0, s] + head + tail
+        f3[0, s] = f3[0, s] + flat[704 + s * 32 : 736 + s * 32, :]
 
     def emit(dst, high):
         for blk in range(4):
@@ -425,28 +453,28 @@
 def on_device(volume):
     w = jnp.asarray(column_weights(), bf16)
     we = jnp.asarray(edge_weights(), bf16)
-    ws = jnp.asarray(shell_weights(), bf16)
     buf = pltpu.VMEM
-    shells = pl.pallas_call(
+    levels = [buf((10, 80, 128), f32), buf((7, 48, 128), f32), buf((5, 32, 128), f32)]
+    shells, volume = call(
         shell_kernel,
-        grid=(1,),
-        out_shape=shape(8, 1024),
-        in_specs=[
-            pl.BlockSpec((16, 64, 128), lambda i: (0, 0, 0)),
-            pl.BlockSpec((16, 64, 128), lambda i: (0, 0, 7)),
-            pl.BlockSpec((16, 256), lambda i: (0, 0)),
-        ],
-        out_specs=pl.BlockSpec((8, 1024), lambda i: (0, 0)),
-        compiler_params=pltpu.CompilerParams(vmem_limit_bytes=8 << 20),
-        cost_estimate=pl.CostEstimate(flops=10**8, bytes_accessed=1 << 20, transcendentals=0),
-        name="shells",
-    )(volume, volume, ws)
+        [shape(24, 128), shape(16, 64, 1024)],
+        [buf((16, 64, 128), f32)]
+        + [buf((768, 256), bf16), buf((1024, 768), bf16), buf((1024, 256), f32)]
+        + levels
+        + [buf((896, 128), f32), pltpu.SemaphoreType.DMA((3,))],
+        (volume,),
+        "shells",
+        10**8,
+        1 << 20,
+        specs=[pl.BlockSpec(memory_space=pltpu.HBM)],
+        limit=48,
+    )
     xa = swap(shells, "gx", 0)
     block = [buf((2, 10, 80, 128), f32), buf((2, 10, 48, 128), f32), buf((480, 768), bf16), buf((480, 256), f32)]
     e, f2s, f3s = shape(2, 10, 48, 128), shape(2, 7, 32, 128), shape(1, 5, 32, 128)
     ea, side, again = call(
         first_kernel,
-        [e, shape(10, 48, 128), shape(8, 1024)],
+        [e, shape(10, 48, 128), shape(24, 128)],
         block,
         (volume, w, shells),
         "first",
@@ -473,8 +501,7 @@
     ea, eb, f2, f3, ya, yb = call(
         columns_kernel,
         [e, e, f2s, f3s, shape(80, 128), shape(80, 128)],
-        [buf((16, 64, 128), f32), buf((10, 80, 128), f32), buf((10, 48, 128), f32), buf((7, 48, 128), f32)]
-        + [buf((7, 32, 128), f32), buf((5, 32, 128), f32), buf((5, 32, 128), f32)],
+        [buf((896, 128), f32)],
         (xa, xb, ea, eb, f2, f3),
         "columns",
         10**8,

time: 33.4 us -> 32 us (0.958)
  local copies, waits for them, and re-layouts: 4.56 us -> 0.01 us
  Pallas kernels: 6.05 us -> 7.75 us
  starting transfers between devices: 14.2 us -> 15.6 us
    unnamed x10 -> x4, local copies, waits for them, and re-layouts: 4.56 us -> 0.01 us
    pallas_call x5 -> x6, Pallas kernels: 5.54 us -> 7.75 us  [call(): pl.pallas_call(kernel, out_shape=outs, in_specs=specs or [VMEM] * len(arg...]
    ppermute x6, starting transfers between devices: 14.2 us -> 15.6 us  [swap(): return lax.ppermute(x, axis, pairs)]
    pallas_call x1 -> x0, Pallas kernels: 0.51 us -> none  [on_device(): pl.pallas_call(shell_kernel, grid=(1,), out_shape=shape(8, 1024), in_spec...]
  transfers between devices with their start and end apart: 6 -> 6, of which waited for: 2 -> 2; matrix products, arithmetic and copies ran while one was open for 0% -> 0% of each run, Pallas kernels for 12% -> 13%
where the time goes in v3:
time: 32 us; the launch traced here: 31.8 us
  starting transfers between devices  15.6 us (49%)
  Pallas kernels  7.75 us (24%)
  waiting for transfers between devices  7.67 us (24%)
  between operations  0.77 us (2%)
    ppermute x6, starting transfers between devices, swap(): return lax.ppermute(x, axis, pairs)  15.6 us
    pallas_call x6, Pallas kernels, call(): pl.pallas_call(kernel, out_shape=outs, in_specs=specs or [VMEM] * len(arg...  7.75 us
    ppermute x6, waiting for transfers between devices, swap(): return lax.ppermute(x, axis, pairs)  7.67 us
  transfers between devices with their start and end apart: 6, of which 2 were waited for; matrix products, arithmetic and copies ran while one was open for 0% of the time, Pallas kernels for 13%

profile of v3, /device:TPU:85, one launch (start us, length us, event | category | flops | bytes accessed | tf_op | source)
XLA Modules:
  0.0 31.8 jit_solution(5046877127884116772)
XLA Ops:
  0.6 0.0 copy-start
  0.6 2.3 %shells.1 = (f32[24,128]{1,0:T(8,128)S(1)}, f32[16,64,1024]{2,1,0:T(8,128)S(1)}) custom-call(f32[16,64,1024]{2,1,0:T(8,128)} %volume.1), custom_call_target="tpu_custom_call" | custom-call | flops 100000000 | bytes 1048576 | tf_op jit(solution)/shard_map/shells/pallas_call | solution.py:440
  3.0 0.1 collective-permute-start
  3.1 0.0 copy-done
  3.1 0.0 copy-start.1
  3.1 1.5 %first.1 = (f32[2,10,48,128]{3,2,1,0:T(8,128)S(1)}, f32[10,48,128]{2,1,0:T(8,128)S(1)}, f32[24,128]{1,0:T(8,128)S(1)}) custom-call(f32[16,64,1024]{2,1,0:T(8,128)S(1)} %get-tuple-element.25.volume, bf16[768,256]{1,0:T(8,128)(2,1)S(1)} %copy-done, f32[24,128]{1,0:T(8,128)S(1)} %get-tuple-element.24.shells), custom_call_target="tpu_custom_call" | custom-call | flops 4000000000 | bytes 2097152 | tf_op jit(solution)/shard_map/first/pallas_call | solution.py:440
  4.5 7.3 %collective-permute-start.1 = (f32[24,128]{1,0:T(8,128)S(1)}, f32[24,128]{1,0:T(8,128)S(1)}, u32[]{:S(2)}, u32[]{:S(2)}) collective-permute-start(f32[24,128]{1,0:T(8,128)S(1)} %get-tuple-element.26), channel_id=1, source_target_pairs={{64,128},{128,64},{65,129},{129,65},{66,130},{130,66},{67,131},{13... | collective-permute-start | bytes 36872 | tf_op jit(solution)/shard_map/ppermute | solution.py:436
  11.8 0.0 copy-done.1
  11.8 2.7 %second.1 = (f32[2,10,48,128]{3,2,1,0:T(8,128)S(1)}, f32[2,10,48,128]{3,2,1,0:T(8,128)S(1)}, f32[2,7,32,128]{3,2,1,0:T(8,128)S(1)}, f32[1,5,32,128]{3,2,1,0:T(8,128)S(1)}) custom-call(f32[16,64,1024]{2,1,0:T(8,128)S(1)} %get-tuple-element.25.volume, bf16[768,256]{1,0:T(8,128)(2,1)S(1)} %copy-done, ...), custom_call_target="tpu_custom_call", output_to_operand_aliasing={{0}: (3, {})} | custom-call | flops 5000000000 | bytes 2097152 | tf_op jit(solution)/shard_map/second/pallas_call | solution.py:440
  14.6 0.0 collective-permute-done.pa
  14.6 0.0 collective-permute-done.1.pb
  14.6 0.3 columns.1
  14.9 1.1 %collective-permute-start.2 = (f32[80,128]{1,0:T(8,128)S(1)}, f32[80,128]{1,0:T(8,128)S(1)}, u32[]{:S(2)}, u32[]{:S(2)}) collective-permute-start(f32[80,128]{1,0:T(8,128)S(1)} %get-tuple-element.33), channel_id=1, source_target_pairs={{0,16},{16,0},{32,48},{48,32},{1,17},{17,1},{33,49},{49,33},{2,18}... | collective-permute-start | bytes 122888 | tf_op jit(solution)/shard_map/ppermute | solution.py:436
  15.9 1.9 %collective-permute-start.3 = (f32[80,128]{1,0:T(8,128)S(1)}, f32[80,128]{1,0:T(8,128)S(1)}, u32[]{:S(2)}, u32[]{:S(2)}) collective-permute-start(f32[80,128]{1,0:T(8,128)S(1)} %get-tuple-element.34), channel_id=1, source_target_pairs={{16,32},{32,16},{17,33},{33,17},{18,34},{34,18},{19,35},{35,19},{2... | collective-permute-start | bytes 122888 | tf_op jit(solution)/shard_map/ppermute | solution.py:436
  17.8 0.0 collective-permute-done.2.pa
  17.9 2.8 %collective-permute-done.3.pb = f32[80,128]{1,0:T(8,128)S(1)} collective-permute-done((f32[80,128]{1,0:T(8,128)S(1)}, f32[80,128]{1,0:T(8,128)S(1)}, u32[]{:S(2)}, u32[]{:S(2)}) %collective-permute-start.3) | collective-permute-done | bytes 40992 | tf_op jit(solution)/shard_map/ppermute | solution.py:436
  20.7 0.1 rows.1
  20.8 2.8 %collective-permute-start.4 = (f32[208,128]{1,0:T(8,128)S(1)}, f32[208,128]{1,0:T(8,128)S(1)}, u32[]{:S(2)}, u32[]{:S(2)}) collective-permute-start(f32[208,128]{1,0:T(8,128)S(1)} %get-tuple-element.39), channel_id=1, source_target_pairs={{0,1},{1,0},{2,3},{3,2},{4,5},{5,4},{6,7},{7,6},{8,9},{9,8},{10,11... | collective-permute-start | bytes 319496 | tf_op jit(solution)/shard_map/ppermute | solution.py:436
  23.5 2.5 %collective-permute-start.5 = (f32[208,128]{1,0:T(8,128)S(1)}, f32[208,128]{1,0:T(8,128)S(1)}, u32[]{:S(2)}, u32[]{:S(2)}) collective-permute-start(f32[208,128]{1,0:T(8,128)S(1)} %get-tuple-element.40), channel_id=1, source_target_pairs={{1,2},{2,1},{3,4},{4,3},{5,6},{6,5},{7,8},{8,7},{9,10},{10,9},{11,... | collective-permute-start | bytes 319496 | tf_op jit(solution)/shard_map/ppermute | solution.py:436
  26.1 0.0 collective-permute-done.4.pa
  26.1 4.9 %collective-permute-done.5.pb = f32[208,128]{1,0:T(8,128)S(1)} collective-permute-done((f32[208,128]{1,0:T(8,128)S(1)}, f32[208,128]{1,0:T(8,128)S(1)}, u32[]{:S(2)}, u32[]{:S(2)}) %collective-permute-start.5) | collective-permute-done | bytes 106528 | tf_op jit(solution)/shard_map/ppermute | solution.py:436
  30.9 0.9 %sections.1 = (f32[8,32,512]{2,1,0:T(8,128)}, f32[4,16,256]{2,1,0:T(8,128)}, f32[2,8,128]{2,1,0:T(8,128)}) custom-call(f32[208,128]{1,0:T(8,128)S(1)} %collective-permute-done.4.pa, f32[208,128]{1,0:T(8,128)S(1)} %collective-permute-done.5.pb, f32[2,10,48,128]{3,2,1,0:T(8,128)S(1)} %get-tuple-element.41.ea, f32[2,10,48,128]{3,2,1,0:T(8,128)S(1)} %get-tuple-element.42.eb, ...), custom_call_target="tpu_custom_call" | custom-call | flops 100000000 | bytes 1048576 | tf_op jit(solution)/shard_map/sections/pallas_call | solution.py:440
Async XLA Ops:
  0.6 2.4 %copy-start = (bf16[768,256]{1,0:T(8,128)(2,1)S(1)}, bf16[768,256]{1,0:T(8,128)(2,1)}, u32[]{:S(2)}) copy-start(bf16[768,256]{1,0:T(8,128)(2,1)} %constant.4.clone.w) | copy-start | bytes 1179652
  3.0 11.6 %collective-permute-start = (f32[24,128]{1,0:T(8,128)S(1)}, f32[24,128]{1,0:T(8,128)S(1)}, u32[]{:S(2)}, u32[]{:S(2)}) collective-permute-start(f32[24,128]{1,0:T(8,128)S(1)} %get-tuple-element.24.shells), channel_id=1, source_target_pairs={{0,64},{64,0},{128,192},{192,128},{1,65},{65,1},{129,193},{193,129... | collective-permute-start | bytes 36872 | tf_op jit(solution)/shard_map/ppermute | solution.py:436
  3.1 8.8 %copy-start.1 = (bf16[384,256]{1,0:T(8,128)(2,1)S(1)}, bf16[384,256]{1,0:T(8,128)(2,1)}, u32[]{:S(2)}) copy-start(bf16[384,256]{1,0:T(8,128)(2,1)} %constant.5.clone.we) | copy-start | bytes 589828
  4.5 10.0 %collective-permute-start.1 = (f32[24,128]{1,0:T(8,128)S(1)}, f32[24,128]{1,0:T(8,128)S(1)}, u32[]{:S(2)}, u32[]{:S(2)}) collective-permute-start(f32[24,128]{1,0:T(8,128)S(1)} %get-tuple-element.26), channel_id=1, source_target_pairs={{64,128},{128,64},{65,129},{129,65},{66,130},{130,66},{67,131},{13... | collective-permute-start | bytes 36872 | tf_op jit(solution)/shard_map/ppermute | solution.py:436
  14.9 3.0 %collective-permute-start.2 = (f32[80,128]{1,0:T(8,128)S(1)}, f32[80,128]{1,0:T(8,128)S(1)}, u32[]{:S(2)}, u32[]{:S(2)}) collective-permute-start(f32[80,128]{1,0:T(8,128)S(1)} %get-tuple-element.33), channel_id=1, source_target_pairs={{0,16},{16,0},{32,48},{48,32},{1,17},{17,1},{33,49},{49,33},{2,18}... | collective-permute-start | bytes 122888 | tf_op jit(solution)/shard_map/ppermute | solution.py:436
  15.9 4.7 %collective-permute-start.3 = (f32[80,128]{1,0:T(8,128)S(1)}, f32[80,128]{1,0:T(8,128)S(1)}, u32[]{:S(2)}, u32[]{:S(2)}) collective-permute-start(f32[80,128]{1,0:T(8,128)S(1)} %get-tuple-element.34), channel_id=1, source_target_pairs={{16,32},{32,16},{17,33},{33,17},{18,34},{34,18},{19,35},{35,19},{2... | collective-permute-start | bytes 122888 | tf_op jit(solution)/shard_map/ppermute | solution.py:436
  20.8 5.3 %collective-permute-start.4 = (f32[208,128]{1,0:T(8,128)S(1)}, f32[208,128]{1,0:T(8,128)S(1)}, u32[]{:S(2)}, u32[]{:S(2)}) collective-permute-start(f32[208,128]{1,0:T(8,128)S(1)} %get-tuple-element.39), channel_id=1, source_target_pairs={{0,1},{1,0},{2,3},{3,2},{4,5},{5,4},{6,7},{7,6},{8,9},{9,8},{10,11... | collective-permute-start | bytes 319496 | tf_op jit(solution)/shard_map/ppermute | solution.py:436
  23.5 7.4 %collective-permute-start.5 = (f32[208,128]{1,0:T(8,128)S(1)}, f32[208,128]{1,0:T(8,128)S(1)}, u32[]{:S(2)}, u32[]{:S(2)}) collective-permute-start(f32[208,128]{1,0:T(8,128)S(1)} %get-tuple-element.40), channel_id=1, source_target_pairs={{1,2},{2,1},{3,4},{4,3},{5,6},{6,5},{7,8},{8,7},{9,10},{10,9},{11,... | collective-permute-start | bytes 319496 | tf_op jit(solution)/shard_map/ppermute | solution.py:436

commit v4 on v3

--- a/solution.py
+++ b/solution.py
@@ -5,6 +5,7 @@
 from jax.experimental import pallas as pl
 from jax.experimental.pallas import tpu as pltpu
 from jax.sharding import PartitionSpec as P
+
 
 taps = (0.0625, 0.25, 0.375, 0.25, 0.0625)
 f32, bf16 = jnp.float32, jnp.bfloat16
@@ -31,7 +32,7 @@
                 continue
             i = (place + 2 - k) // 2
             if c >= 64:
-                lane = 128 + i if i < 0 else 128 + i
+                lane = 128 + i
                 w[c, lane] += taps[k]
             else:
                 lane = i if i >= 0 else 256 + i
@@ -99,7 +100,7 @@
         store(i, v)
 
 
-def rows(src, dst, at, half, above, ends):
+def rows(src, dst, at, half, ends):
     n = 2 * half
     dst[at, 8 : 8 + half, :] = weigh(
         [src[at, pl.ds(6 + k, half, stride=2), :] for k in range(5)]
@@ -121,10 +122,6 @@
     for j, x in enumerate(parts):
         for q, piece in enumerate(split(x)):
             dst[at : at + tall, q * wide + j * 128 : q * wide + (j + 1) * 128] = piece
-
-
-def lane():
-    return lax.broadcasted_iota(jnp.int32, (8, 128), 1)
 
 
 def low_lanes(tall):
@@ -148,7 +145,7 @@
 
         sections(lambda i, r=r: src[i, r : r + 8, :], store, 0, 15, 8, 1, zend)
     for s in range(10):
-        rows(z1, y1, s, 32, 1, yend)
+        rows(z1, y1, s, 32, yend)
     for a, zb, b, used, first, half_z, half_y in (
         (y1, z2, y2, 48, 8, 4, 16),
         (y2, z3, y3, 32, 5, 2, 8),
@@ -160,7 +157,7 @@
 
             sections(lambda i, r=r, a=a: a[i + 1, r : r + 8, :], store, -1, first, half_z, 2, zend)
         for s in range(half_z + 3):
-            rows(zb, b, s, half_y, 2, yend)
+            rows(zb, b, s, half_y, yend)
 
 
 TALL = ((0, 10, 48), (480, 7, 32), (704, 5, 32))
@@ -222,14 +219,12 @@
             sections(lambda i, r=r, cols=cols: volume[i, r : r + 8, cols], store, 0, 15, 8, 1, zend)
     for s in range(10):
         for h in range(2):
-            rows(zs.at[h], ys.at[h], s, 32, 1, yend)
+            rows(zs.at[h], ys.at[h], s, 32, yend)
         pack([ys[0, s], ys[1, s]], ops, s * 48)
     res[...] = matmul(ops[...], w[...])
 
 
-def first_kernel(volume, w, shells, ea, side, again, zs, ys, ops, res):
-    again[...] = shells[...]
-    zend, yend = keep("gz", lax.axis_size("gz")), keep("gy", lax.axis_size("gy"))
+def first_half(volume, w, ea, side, zs, ys, ops, res, zend, yend):
     low = low_lanes(48)
     for b in range(2):
         level_one_block(volume, b, zs, ys, ops, res, w, zend, yend)
@@ -246,8 +241,21 @@
                 side[s] = jnp.where(low, beside, first)
 
 
+def early():
+    return lax.axis_index("gx") < lax.axis_size("gx") // 2
+
+
+def first_kernel(volume, w, shells, ea, side, again, zs, ys, ops, res):
+    again[...] = shells[...]
+    zend, yend = keep("gz", lax.axis_size("gz")), keep("gy", lax.axis_size("gy"))
+
+    @pl.when(early())
+    def _():
+        first_half(volume, w, ea, side, zs, ys, ops, res, zend, yend)
+
+
 def next_level(blocks, edge, zs, ys, ops, edge_ops, res, edge_res, w, we, dst, edge_dst,
-               sections_in, half_z, half_y, tall_in, used_in, tall, zend, yend, xend):
+               sections_in, half_z, half_y, used_in, tall, zend, yend, xend):
     count = len(blocks)
     many = half_z + 3
     for j, src in enumerate(blocks + [edge]):
@@ -259,7 +267,7 @@
             sections(lambda i, r=r, src=src: src[i + 1, r : r + 8, :], store, -1,
                      sections_in - 2, half_z, 2, zend)
         for s in range(many):
-            rows(zs.at[j], ys.at[j], s, half_y, 2, yend)
+            rows(zs.at[j], ys.at[j], s, half_y, yend)
     size = many * tall
     for p in range(count // 2):
         for s in range(many):
@@ -287,11 +295,16 @@
             edge_dst[s] = wrapped * jnp.where(low, xend[1], xend[0])
 
 
-def second_kernel(volume, w, we, ea_in, side, ea, eb, f2, f3,
+def second_kernel(volume, w, we, ea_in, side_in, ea, side, eb, f2, f3,
                   zs, ys, ops, res, h1, z2, y2, ops2, opse2, res2, rese2, h2,
                   z3, y3, ops3, opse3, res3, rese3):
     zend, yend, xend = (keep(a, lax.axis_size(a)) for a in ("gz", "gy", "gx"))
     low = low_lanes(48)
+
+    @pl.when(jnp.logical_not(early()))
+    def _():
+        first_half(volume, w, ea, side, zs, ys, ops, res, zend, yend)
+
     for b in range(2):
         level_one_block(volume, 2 + b, zs, ys, ops, res, w, zend, yend)
         for s in range(10):
@@ -306,9 +319,9 @@
                 eb[0, s] = eb[0, s] + jnp.where(low, 0.0, beside)
                 h1[s] = jnp.where(low, beside * xend[1], side[s] * xend[0])
     next_level([ea.at[0], ea.at[1], eb.at[0], eb.at[1]], h1, z2, y2, ops2, opse2, res2, rese2,
-               w, we, f2, h2, 10, 4, 16, 48, 48, 32, zend, yend, xend)
+               w, we, f2, h2, 10, 4, 16, 48, 32, zend, yend, xend)
     next_level([f2.at[0], f2.at[1]], h2, z3, y3, ops3, opse3, res3, rese3,
-               w, we, f3, None, 7, 2, 8, 32, 32, 32, zend, yend, xend)
+               w, we, f3, None, 7, 2, 8, 32, 32, zend, yend, xend)
 
 
 def columns_kernel(pa, pb, ea_in, eb_in, f2_in, f3_in, ea, eb, f2, f3, ya, yb, flat):
@@ -354,6 +367,7 @@
 
 def rows_kernel(pa, pb, ea_in, eb_in, f2_in, f3_in, ea, eb, f2, f3, za, zb):
     odd = lax.rem(lax.axis_index("gy"), 2) == 1
+
     def got(at):
         a, b = pa[at : at + 1, :], pb[at : at + 1, :]
         return jnp.where(odd, a, b), jnp.where(odd, b, a)
@@ -436,7 +450,7 @@
     return lax.ppermute(x, axis, pairs)
 
 
-def call(kernel, outs, scratch, args, name, flops, moved, specs=None, aliases=None, limit=16):
+def call(kernel, outs, scratch, args, flops, moved, specs=None, aliases=None, limit=16):
     return pl.pallas_call(
         kernel,
         out_shape=outs,
@@ -446,7 +460,6 @@
         input_output_aliases=aliases or {},
         compiler_params=pltpu.CompilerParams(vmem_limit_bytes=limit << 20),
         cost_estimate=pl.CostEstimate(flops=flops, bytes_accessed=moved, transcendentals=0),
-        name=name,
     )(*args)
 
 
@@ -463,7 +476,6 @@
         + levels
         + [buf((896, 128), f32), pltpu.SemaphoreType.DMA((3,))],
         (volume,),
-        "shells",
         10**8,
         1 << 20,
         specs=[pl.BlockSpec(memory_space=pltpu.HBM)],
@@ -477,14 +489,13 @@
         [e, shape(10, 48, 128), shape(24, 128)],
         block,
         (volume, w, shells),
-        "first",
         4 * 10**9,
         1 << 21,
     )
     xb = swap(again, "gx", 1)
-    ea, eb, f2, f3 = call(
+    ea, _, eb, f2, f3 = call(
         second_kernel,
-        [e, e, f2s, f3s],
+        [e, shape(10, 48, 128), e, f2s, f3s],
         block
         + [buf((10, 48, 128), f32)]
         + [buf((5, 7, 48, 128), f32), buf((5, 7, 32, 128), f32), buf((448, 768), bf16), buf((224, 384), bf16)]
@@ -492,10 +503,9 @@
         + [buf((3, 5, 32, 128), f32), buf((3, 5, 32, 128), f32), buf((160, 768), bf16), buf((160, 384), bf16)]
         + [buf((160, 256), f32), buf((160, 256), f32)],
         (volume, w, we, ea, side),
-        "second",
         5 * 10**9,
         1 << 21,
-        aliases={3: 0},
+        aliases={3: 0, 4: 1},
     )
     keepers = {2: 0, 3: 1, 4: 2, 5: 3}
     ea, eb, f2, f3, ya, yb = call(
@@ -503,7 +513,6 @@
         [e, e, f2s, f3s, shape(80, 128), shape(80, 128)],
         [buf((896, 128), f32)],
         (xa, xb, ea, eb, f2, f3),
-        "columns",
         10**8,
         1 << 20,
         aliases=keepers,
@@ -514,19 +523,18 @@
         [e, e, f2s, f3s, shape(208, 128), shape(208, 128)],
         [],
         (ya, yb, ea, eb, f2, f3),
-        "rows",
         10**8,
         1 << 20,
         aliases=keepers,
     )
-    za, zb = swap(za, "gz", 0), swap(zb, "gz", 1)
+    zb = swap(zb, "gz", 1)
+    za = swap(za, "gz", 0)
     return tuple(
         call(
             sections_kernel,
             [shape(8, 32, 512), shape(4, 16, 256), shape(2, 8, 128)],
             [],
             (za, zb, ea, eb, f2, f3),
-            "sections",
             10**8,
             1 << 20,
         )

time: 32 us -> 30.7 us (0.959)
  starting transfers between devices: 15.6 us -> 14.3 us
    ppermute x6, starting transfers between devices: 15.6 us -> 14.3 us  [swap(): return lax.ppermute(x, axis, pairs)]
  transfers between devices with their start and end apart: 6 -> 6, of which waited for: 2 -> 2; matrix products, arithmetic and copies ran while one was open for 0% -> 0% of each run, Pallas kernels for 13% -> 14%
where the time goes in v4:
time: 30.7 us; the launch traced here: 30.5 us
  starting transfers between devices  14.3 us (47%)
  Pallas kernels  7.79 us (25%)
  waiting for transfers between devices  7.67 us (25%)
  between operations  0.77 us (3%)
    ppermute x6, starting transfers between devices, swap(): return lax.ppermute(x, axis, pairs)  14.3 us
    pallas_call x6, Pallas kernels, call(): pl.pallas_call(kernel, out_shape=outs, in_specs=specs or [VMEM] * len(arg...  7.79 us
    ppermute x6, waiting for transfers between devices, swap(): return lax.ppermute(x, axis, pairs)  7.67 us
  transfers between devices with their start and end apart: 6, of which 2 were waited for; matrix products, arithmetic and copies ran while one was open for 0% of the time, Pallas kernels for 14%

profile of v4, /device:TPU:85, one launch (start us, length us, event | category | flops | bytes accessed | tf_op | source)
XLA Modules:
  0.0 30.5 jit_solution(3028003332136275372)
XLA Ops:
  0.6 0.0 copy-start
  0.6 2.3 %shard_map.58 = (f32[24,128]{1,0:T(8,128)S(1)}, f32[16,64,1024]{2,1,0:T(8,128)S(1)}) custom-call(f32[16,64,1024]{2,1,0:T(8,128)} %volume.1), custom_call_target="tpu_custom_call" | custom-call | flops 100000000 | bytes 1048576 | tf_op jit(solution)/shard_map/pallas_call | solution.py:454
  3.0 0.1 collective-permute-start
  3.1 0.0 copy-done
  3.1 0.0 copy-start.1
  3.1 1.5 %shard_map.59 = (f32[2,10,48,128]{3,2,1,0:T(8,128)S(1)}, f32[10,48,128]{2,1,0:T(8,128)S(1)}, f32[24,128]{1,0:T(8,128)S(1)}) custom-call(f32[16,64,1024]{2,1,0:T(8,128)S(1)} %get-tuple-element.25.volume, bf16[768,256]{1,0:T(8,128)(2,1)S(1)} %copy-done, f32[24,128]{1,0:T(8,128)S(1)} %get-tuple-element.24.shells), custom_call_target="tpu_custom_call" | custom-call | flops 4000000000 | bytes 2097152 | tf_op jit(solution)/shard_map/pallas_call | solution.py:454
  4.5 5.9 %collective-permute-start.1 = (f32[24,128]{1,0:T(8,128)S(1)}, f32[24,128]{1,0:T(8,128)S(1)}, u32[]{:S(2)}, u32[]{:S(2)}) collective-permute-start(f32[24,128]{1,0:T(8,128)S(1)} %get-tuple-element.26), channel_id=1, source_target_pairs={{64,128},{128,64},{65,129},{129,65},{66,130},{130,66},{67,131},{13... | collective-permute-start | bytes 36872 | tf_op jit(solution)/shard_map/ppermute | solution.py:450
  10.5 0.0 copy-done.1
  10.5 2.8 %shard_map.60 = (f32[2,10,48,128]{3,2,1,0:T(8,128)S(1)}, f32[10,48,128]{2,1,0:T(8,128)S(1)}, f32[2,10,48,128]{3,2,1,0:T(8,128)S(1)}, f32[2,7,32,128]{3,2,1,0:T(8,128)S(1)}, f32[1,5,32,128]{3,2,1,0:T(8,128)S(1)}) custom-call(f32[16,64,1024]{2,1,0:T(8,128)S(1)} %get-tuple-element.25.volume, ...), custom_call_target="tpu_custom_call", output_to_operand_aliasing={{0}: (3, {}), {1}: (4, {})} | custom-call | flops 5000000000 | bytes 2097152 | tf_op jit(solution)/shard_map/pallas_call | solution.py:454
  13.3 0.0 collective-permute-done.pa
  13.3 0.0 collective-permute-done.1.pb
  13.3 0.3 shard_map.61
  13.6 1.1 %collective-permute-start.2 = (f32[80,128]{1,0:T(8,128)S(1)}, f32[80,128]{1,0:T(8,128)S(1)}, u32[]{:S(2)}, u32[]{:S(2)}) collective-permute-start(f32[80,128]{1,0:T(8,128)S(1)} %get-tuple-element.33), channel_id=1, source_target_pairs={{0,16},{16,0},{32,48},{48,32},{1,17},{17,1},{33,49},{49,33},{2,18}... | collective-permute-start | bytes 122888 | tf_op jit(solution)/shard_map/ppermute | solution.py:450
  14.6 1.9 %collective-permute-start.3 = (f32[80,128]{1,0:T(8,128)S(1)}, f32[80,128]{1,0:T(8,128)S(1)}, u32[]{:S(2)}, u32[]{:S(2)}) collective-permute-start(f32[80,128]{1,0:T(8,128)S(1)} %get-tuple-element.34), channel_id=1, source_target_pairs={{16,32},{32,16},{17,33},{33,17},{18,34},{34,18},{19,35},{35,19},{2... | collective-permute-start | bytes 122888 | tf_op jit(solution)/shard_map/ppermute | solution.py:450
  16.5 0.0 collective-permute-done.2.pa
  16.6 2.8 %collective-permute-done.3.pb = f32[80,128]{1,0:T(8,128)S(1)} collective-permute-done((f32[80,128]{1,0:T(8,128)S(1)}, f32[80,128]{1,0:T(8,128)S(1)}, u32[]{:S(2)}, u32[]{:S(2)}) %collective-permute-start.3) | collective-permute-done | bytes 40992 | tf_op jit(solution)/shard_map/ppermute | solution.py:450
  19.4 0.1 shard_map.62
  19.5 2.8 %collective-permute-start.4 = (f32[208,128]{1,0:T(8,128)S(1)}, f32[208,128]{1,0:T(8,128)S(1)}, u32[]{:S(2)}, u32[]{:S(2)}) collective-permute-start(f32[208,128]{1,0:T(8,128)S(1)} %get-tuple-element.39), channel_id=1, source_target_pairs={{0,1},{1,0},{2,3},{3,2},{4,5},{5,4},{6,7},{7,6},{8,9},{9,8},{10,11... | collective-permute-start | bytes 319496 | tf_op jit(solution)/shard_map/ppermute | solution.py:450
  22.2 2.5 %collective-permute-start.5 = (f32[208,128]{1,0:T(8,128)S(1)}, f32[208,128]{1,0:T(8,128)S(1)}, u32[]{:S(2)}, u32[]{:S(2)}) collective-permute-start(f32[208,128]{1,0:T(8,128)S(1)} %get-tuple-element.40), channel_id=1, source_target_pairs={{1,2},{2,1},{3,4},{4,3},{5,6},{6,5},{7,8},{8,7},{9,10},{10,9},{11,... | collective-permute-start | bytes 319496 | tf_op jit(solution)/shard_map/ppermute | solution.py:450
  24.8 0.0 collective-permute-done.4.pa
  24.8 4.9 %collective-permute-done.5.pb = f32[208,128]{1,0:T(8,128)S(1)} collective-permute-done((f32[208,128]{1,0:T(8,128)S(1)}, f32[208,128]{1,0:T(8,128)S(1)}, u32[]{:S(2)}, u32[]{:S(2)}) %collective-permute-start.5) | collective-permute-done | bytes 106528 | tf_op jit(solution)/shard_map/ppermute | solution.py:450
  29.6 0.9 %shard_map.63 = (f32[8,32,512]{2,1,0:T(8,128)}, f32[4,16,256]{2,1,0:T(8,128)}, f32[2,8,128]{2,1,0:T(8,128)}) custom-call(f32[208,128]{1,0:T(8,128)S(1)} %collective-permute-done.4.pa, f32[208,128]{1,0:T(8,128)S(1)} %collective-permute-done.5.pb, f32[2,10,48,128]{3,2,1,0:T(8,128)S(1)} %get-tuple-element.41.ea, f32[2,10,48,128]{3,2,1,0:T(8,128)S(1)} %get-tuple-element.42.eb, ...), custom_call_target="tpu_custom_call" | custom-call | flops 100000000 | bytes 1048576 | tf_op jit(solution)/shard_map/pallas_call | solution.py:454
Async XLA Ops:
  0.6 2.4 %copy-start = (bf16[768,256]{1,0:T(8,128)(2,1)S(1)}, bf16[768,256]{1,0:T(8,128)(2,1)}, u32[]{:S(2)}) copy-start(bf16[768,256]{1,0:T(8,128)(2,1)} %constant.4.clone.w) | copy-start | bytes 1179652
  3.0 10.3 %collective-permute-start = (f32[24,128]{1,0:T(8,128)S(1)}, f32[24,128]{1,0:T(8,128)S(1)}, u32[]{:S(2)}, u32[]{:S(2)}) collective-permute-start(f32[24,128]{1,0:T(8,128)S(1)} %get-tuple-element.24.shells), channel_id=1, source_target_pairs={{0,64},{64,0},{128,192},{192,128},{1,65},{65,1},{129,193},{193,129... | collective-permute-start | bytes 36872 | tf_op jit(solution)/shard_map/ppermute | solution.py:450
  3.1 7.4 %copy-start.1 = (bf16[384,256]{1,0:T(8,128)(2,1)S(1)}, bf16[384,256]{1,0:T(8,128)(2,1)}, u32[]{:S(2)}) copy-start(bf16[384,256]{1,0:T(8,128)(2,1)} %constant.5.clone.we) | copy-start | bytes 589828
  4.5 8.7 %collective-permute-start.1 = (f32[24,128]{1,0:T(8,128)S(1)}, f32[24,128]{1,0:T(8,128)S(1)}, u32[]{:S(2)}, u32[]{:S(2)}) collective-permute-start(f32[24,128]{1,0:T(8,128)S(1)} %get-tuple-element.26), channel_id=1, source_target_pairs={{64,128},{128,64},{65,129},{129,65},{66,130},{130,66},{67,131},{13... | collective-permute-start | bytes 36872 | tf_op jit(solution)/shard_map/ppermute | solution.py:450
  13.6 3.0 %collective-permute-start.2 = (f32[80,128]{1,0:T(8,128)S(1)}, f32[80,128]{1,0:T(8,128)S(1)}, u32[]{:S(2)}, u32[]{:S(2)}) collective-permute-start(f32[80,128]{1,0:T(8,128)S(1)} %get-tuple-element.33), channel_id=1, source_target_pairs={{0,16},{16,0},{32,48},{48,32},{1,17},{17,1},{33,49},{49,33},{2,18}... | collective-permute-start | bytes 122888 | tf_op jit(solution)/shard_map/ppermute | solution.py:450
  14.6 4.7 %collective-permute-start.3 = (f32[80,128]{1,0:T(8,128)S(1)}, f32[80,128]{1,0:T(8,128)S(1)}, u32[]{:S(2)}, u32[]{:S(2)}) collective-permute-start(f32[80,128]{1,0:T(8,128)S(1)} %get-tuple-element.34), channel_id=1, source_target_pairs={{16,32},{32,16},{17,33},{33,17},{18,34},{34,18},{19,35},{35,19},{2... | collective-permute-start | bytes 122888 | tf_op jit(solution)/shard_map/ppermute | solution.py:450
  19.5 5.3 %collective-permute-start.4 = (f32[208,128]{1,0:T(8,128)S(1)}, f32[208,128]{1,0:T(8,128)S(1)}, u32[]{:S(2)}, u32[]{:S(2)}) collective-permute-start(f32[208,128]{1,0:T(8,128)S(1)} %get-tuple-element.39), channel_id=1, source_target_pairs={{0,1},{1,0},{2,3},{3,2},{4,5},{5,4},{6,7},{7,6},{8,9},{9,8},{10,11... | collective-permute-start | bytes 319496 | tf_op jit(solution)/shard_map/ppermute | solution.py:450
  22.2 7.4 %collective-permute-start.5 = (f32[208,128]{1,0:T(8,128)S(1)}, f32[208,128]{1,0:T(8,128)S(1)}, u32[]{:S(2)}, u32[]{:S(2)}) collective-permute-start(f32[208,128]{1,0:T(8,128)S(1)} %get-tuple-element.40), channel_id=1, source_target_pairs={{1,2},{2,1},{3,4},{4,3},{5,6},{6,5},{7,8},{8,7},{9,10},{10,9},{11,... | collective-permute-start | bytes 319496 | tf_op jit(solution)/shard_map/ppermute | solution.py:450

commit v5 on v4

--- a/solution.py
+++ b/solution.py
@@ -12,32 +12,33 @@
 VMEM = pl.BlockSpec(memory_space=pltpu.VMEM)
 
 
-def column_weights():
-    w = np.zeros((256, 256), np.float32)
-    for i in range(-1, 129):
-        for k in range(5):
-            c = 2 * i - 2 + k
-            if 0 <= c < 256:
-                lane = i if 0 <= i < 128 else (128 if i == 128 else 255)
-                w[c, lane] += taps[k]
-    return np.concatenate([w] * 3, axis=0)
-
-
-def edge_weights():
-    w = np.zeros((128, 256), np.float32)
-    for c in range(128):
-        for k in range(5):
-            place = c - 128 if c >= 64 else c
-            if (place + 2 - k) % 2:
-                continue
-            i = (place + 2 - k) // 2
-            if c >= 64:
-                lane = 128 + i
-                w[c, lane] += taps[k]
-            else:
-                lane = i if i >= 0 else 256 + i
-                w[c, lane] += taps[k]
-    return np.concatenate([w] * 3, axis=0)
+def tap(k):
+    outer, inner = (k == 0) | (k == 4), (k == 1) | (k == 3)
+    return jnp.where(outer, taps[0], jnp.where(inner, taps[1], jnp.where(k == 2, taps[2], 0.0)))
+
+
+def reduce_weights(w, wrap):
+    lane_at = lax.broadcasted_iota(jnp.int32, (128, 128), 1)
+    row = lax.broadcasted_iota(jnp.int32, (128, 128), 0)
+
+    def beside(c, n):
+        under = jnp.where(lane_at == 0, tap(c - n + 2), 0.0)
+        return jnp.where(lane_at == 127, jnp.where(c == 0, taps[4], 0.0), under)
+
+    for h in range(2):
+        c = row + h * 128
+        main, out = tap(c - 2 * lane_at + 2).astype(bf16), beside(c, 256).astype(bf16)
+        for q in range(3):
+            at = q * 256 + h * 128
+            w[at : at + 128, 0:128] = main
+            w[at : at + 128, 128:256] = out
+    high = (row >= 64) & (lane_at >= 64)
+    low = (row < 64) & (lane_at < 64)
+    k = jnp.where(high, row - 2 * lane_at + 130, jnp.where(low, row - 2 * lane_at + 2, -1))
+    main, out = tap(k).astype(bf16), beside(row, 128).astype(bf16)
+    for q in range(3):
+        wrap[q * 128 : q * 128 + 128, 0:128] = main
+        wrap[q * 128 : q * 128 + 128, 128:256] = out
 
 
 def composite(levels):
@@ -164,27 +165,28 @@
 MIXED = ((3, 96), (5, 64))
 
 
-def shell_kernel(volume, out, kept, own, w, lines, prod, z1, z2, z3, flat, sems):
+def shell_kernel(volume, out, reduce_w, wrap_w, left, right, own, w, lines, prod, z1, z2, z3, flat, sems):
     copies = []
-    for j, (first, wide) in enumerate(((0, 128), (896, 128), (128, 768))):
-        cols = pl.ds(first, wide)
-        copies.append(pltpu.make_async_copy(volume.at[:, :, cols], kept.at[:, :, cols], sems.at[j]))
+    for j, (first, dst) in enumerate(((0, left), (896, right))):
+        copies.append(pltpu.make_async_copy(volume.at[:, :, pl.ds(first, 128)], dst, sems.at[j]))
     for c in copies:
         c.start()
     zend, yend = keep("gz", lax.axis_size("gz")), keep("gy", lax.axis_size("gy"))
-    w[...] = jnp.zeros((768, 256), bf16)
-    for first in (0, 240):
+    reduce_weights(reduce_w, wrap_w)
+    w[...] = jnp.zeros((384, 256), bf16)
+    for first, to in ((0, 0), (240, 112)):
         for j, part in enumerate(shell_weights(first, 16)):
             for q in range(3):
-                w[q * 256 + first : q * 256 + first + 16, j * 128 : j * 128 + 128] = part
+                w[q * 128 + to : q * 128 + to + 16, j * 128 : j * 128 + 128] = part
     for s in range(5):
         flat[704 + s * 32 + 24 : 704 + s * 32 + 32, :] = jnp.zeros((8, 128), f32)
     flat[864:896, :] = jnp.zeros((32, 128), f32)
     out[16:24, :] = jnp.zeros((8, 128), f32)
     copies[0].wait()
     copies[1].wait()
+    low = low_lanes(64)
     for s in range(16):
-        pack([kept[s, :, 0:128], kept[s, :, 896:1024]], lines, s * 64)
+        pack([jnp.where(low, left[s], right[s])], lines, s * 64)
     prod[...] = matmul(lines[...], w[...])
     for s in range(16):
         lines_s = prod[s * 64 : s * 64 + 64, :]
@@ -202,7 +204,6 @@
             if j in mixed:
                 row = jnp.where(at < mixed[j], row, pick[level + 1][q])
             out[3 * j + q : 3 * j + q + 1, :] = row
-    copies[2].wait()
 
 
 def level_one_block(volume, at, zs, ys, ops, res, w, zend, yend):
@@ -411,7 +412,17 @@
         pl.when(jnp.logical_not(when))(lambda dst=dst: emit(dst, True))
 
 
-def sections_kernel(pa, pb, ea, eb, f2, f3, one, two, three):
+def inner_kernel(ea, eb, one, held, sem):
+    for blk in range(4):
+        e = ea if blk < 2 else eb
+        for z in range(1, 7):
+            held[z - 1, :, blk * 128 : blk * 128 + 128] = e[blk % 2, z + 1, 8:40, :]
+    copy = pltpu.make_async_copy(held, one.at[pl.ds(1, 6)], sem)
+    copy.start()
+    copy.wait()
+
+
+def sections_kernel(pa, pb, ea, eb, f2, f3, one_in, one, two_out, three_out, held, two, three, sems):
     odd = lax.rem(lax.axis_index("gz"), 2) == 1
 
     def got(at, tall):
@@ -421,10 +432,12 @@
     for blk in range(4):
         e = ea if blk < 2 else eb
         under, over = got(blk * 32, 32)
-        for z in range(8):
-            v = e[blk % 2, z + 1, 8:40, :]
-            v = v + under if z == 0 else v + over if z == 7 else v
-            one[z, :, blk * 128 : blk * 128 + 128] = v
+        cols = slice(blk * 128, blk * 128 + 128)
+        held[0, :, cols] = e[blk % 2, 1, 8:40, :] + under
+        held[1, :, cols] = e[blk % 2, 8, 8:40, :] + over
+    copies = [pltpu.make_async_copy(held.at[j], one.at[7 * j], sems.at[j]) for j in range(2)]
+    for c in copies:
+        c.start()
     for blk in range(2):
         under, over = got(128 + blk * 16, 16)
         further, _ = got(160 + blk * 16, 16)
@@ -436,6 +449,14 @@
     further, _ = got(200, 8)
     three[0] = f3[0, 1, 8:16, :] + under
     three[1] = f3[0, 2, 8:16, :] + further + over
+    copies += [
+        pltpu.make_async_copy(two, two_out, sems.at[2]),
+        pltpu.make_async_copy(three, three_out, sems.at[3]),
+    ]
+    for c in copies[2:]:
+        c.start()
+    for c in copies:
+        c.wait()
 
 
 def shape(*dims):
@@ -450,12 +471,12 @@
     return lax.ppermute(x, axis, pairs)
 
 
-def call(kernel, outs, scratch, args, flops, moved, specs=None, aliases=None, limit=16):
+def call(kernel, outs, scratch, args, flops, moved, specs=None, aliases=None, limit=16, outs_in=None):
     return pl.pallas_call(
         kernel,
         out_shape=outs,
         in_specs=specs or [VMEM] * len(args),
-        out_specs=[VMEM] * len(outs),
+        out_specs=outs_in or [VMEM] * len(outs),
         scratch_shapes=scratch,
         input_output_aliases=aliases or {},
         compiler_params=pltpu.CompilerParams(vmem_limit_bytes=limit << 20),
@@ -464,22 +485,20 @@
 
 
 def on_device(volume):
-    w = jnp.asarray(column_weights(), bf16)
-    we = jnp.asarray(edge_weights(), bf16)
     buf = pltpu.VMEM
     levels = [buf((10, 80, 128), f32), buf((7, 48, 128), f32), buf((5, 32, 128), f32)]
-    shells, volume = call(
+    shells, w, we = call(
         shell_kernel,
-        [shape(24, 128), shape(16, 64, 1024)],
-        [buf((16, 64, 128), f32)]
-        + [buf((768, 256), bf16), buf((1024, 768), bf16), buf((1024, 256), f32)]
+        [shape(24, 128), jax.ShapeDtypeStruct((768, 256), bf16), jax.ShapeDtypeStruct((384, 256), bf16)],
+        [buf((16, 64, 128), f32)] * 3
+        + [buf((384, 256), bf16), buf((1024, 384), bf16), buf((1024, 256), f32)]
         + levels
-        + [buf((896, 128), f32), pltpu.SemaphoreType.DMA((3,))],
+        + [buf((896, 128), f32), pltpu.SemaphoreType.DMA((2,))],
         (volume,),
         10**8,
         1 << 20,
         specs=[pl.BlockSpec(memory_space=pltpu.HBM)],
-        limit=48,
+        limit=50,
     )
     xa = swap(shells, "gx", 0)
     block = [buf((2, 10, 80, 128), f32), buf((2, 10, 48, 128), f32), buf((480, 768), bf16), buf((480, 256), f32)]
@@ -529,14 +548,28 @@
     )
     zb = swap(zb, "gz", 1)
     za = swap(za, "gz", 0)
+    hbm = pl.BlockSpec(memory_space=pltpu.HBM)
+    whole = shape(8, 32, 512)
+    (one,) = call(
+        inner_kernel,
+        [whole],
+        [buf((6, 32, 512), f32), pltpu.SemaphoreType.DMA],
+        (ea, eb),
+        10**8,
+        1 << 20,
+        outs_in=[hbm],
+    )
     return tuple(
         call(
             sections_kernel,
-            [shape(8, 32, 512), shape(4, 16, 256), shape(2, 8, 128)],
-            [],
-            (za, zb, ea, eb, f2, f3),
+            [whole, shape(4, 16, 256), shape(2, 8, 128)],
+            [buf((2, 32, 512), f32), buf((4, 16, 256), f32), buf((2, 8, 128), f32), pltpu.SemaphoreType.DMA((4,))],
+            (za, zb, ea, eb, f2, f3, one),
             10**8,
             1 << 20,
+            specs=[VMEM] * 6 + [hbm],
+            outs_in=[hbm] * 3,
+            aliases={6: 0},
         )
     )
 

time: 30.7 us -> 30.1 us (0.980)
  waiting for transfers between devices: 7.67 us -> 6.86 us
  starting transfers between devices: 14.3 us -> 13.8 us
  Pallas kernels: 7.79 us -> 8.15 us
  local copies, waits for them, and re-layouts: 0.01 us -> 0.37 us
    ppermute x6, waiting for transfers between devices: 7.67 us -> 6.86 us  [swap(): return lax.ppermute(x, axis, pairs)]
    ppermute x6, starting transfers between devices: 14.3 us -> 13.8 us  [swap(): return lax.ppermute(x, axis, pairs)]
    pallas_call x6 -> x7, Pallas kernels: 7.79 us -> 8.15 us  [call(): pl.pallas_call(kernel, out_shape=outs, in_specs=specs or [VMEM] * len(arg...]
    unnamed x4 -> x2, local copies, waits for them, and re-layouts: 0.01 us -> 0.37 us
  transfers between devices with their start and end apart: 6 -> 6, of which waited for: 2 -> 2; matrix products, arithmetic and copies ran while one was open for 0% -> 0% of each run, Pallas kernels for 14% -> 17%
where the time goes in v5:
time: 30.1 us; the launch traced here: 30 us
  starting transfers between devices  13.8 us (46%)
  Pallas kernels  8.15 us (27%)
  waiting for transfers between devices  6.86 us (23%)
  between operations  0.75 us (2%)
  local copies, waits for them, and re-layouts  0.37 us (1%)
    ppermute x6, starting transfers between devices, swap(): return lax.ppermute(x, axis, pairs)  13.8 us
    pallas_call x7, Pallas kernels, call(): pl.pallas_call(kernel, out_shape=outs, in_specs=specs or [VMEM] * len(arg...  8.15 us
    ppermute x6, waiting for transfers between devices, swap(): return lax.ppermute(x, axis, pairs)  6.86 us
  transfers between devices with their start and end apart: 6, of which 2 were waited for; matrix products, arithmetic and copies ran while one was open for 0% of the time, Pallas kernels for 17%

profile of v5, /device:TPU:85, one launch (start us, length us, event | category | flops | bytes accessed | tf_op | source)
XLA Modules:
  0.0 30.0 jit_solution(3361812745071550290)
XLA Ops:
  0.6 0.0 copy-start
  0.6 2.0 %shard_map.38 = (f32[24,128]{1,0:T(8,128)S(1)}, bf16[768,256]{1,0:T(8,128)(2,1)S(1)}, bf16[384,256]{1,0:T(8,128)(2,1)S(1)}) custom-call(f32[16,64,1024]{2,1,0:T(8,128)} %volume.5), custom_call_target="tpu_custom_call" | custom-call | flops 100000000 | bytes 1048576 | tf_op jit(solution)/shard_map/pallas_call | solution.py:475
  2.7 0.1 collective-permute-start
  2.8 0.4 %copy-done = f32[16,64,1024]{2,1,0:T(8,128)S(1)} copy-done((f32[16,64,1024]{2,1,0:T(8,128)S(1)}, f32[16,64,1024]{2,1,0:T(8,128)}, u32[]{:S(2)}) %copy-start) | copy-done | bytes 4194328
  3.1 1.4 %shard_map.39 = (f32[2,10,48,128]{3,2,1,0:T(8,128)S(1)}, f32[10,48,128]{2,1,0:T(8,128)S(1)}, f32[24,128]{1,0:T(8,128)S(1)}) custom-call(f32[16,64,1024]{2,1,0:T(8,128)S(1)} %copy-done, bf16[768,256]{1,0:T(8,128)(2,1)S(1)} %get-tuple-element.26.w, f32[24,128]{1,0:T(8,128)S(1)} %get-tuple-element.25.shells), custom_call_target="tpu_custom_call" | custom-call | flops 4000000000 | bytes 2097152 | tf_op jit(solution)/shard_map/pallas_call | solution.py:475
  4.6 5.5 %collective-permute-start.1 = (f32[24,128]{1,0:T(8,128)S(1)}, f32[24,128]{1,0:T(8,128)S(1)}, u32[]{:S(2)}, u32[]{:S(2)}) collective-permute-start(f32[24,128]{1,0:T(8,128)S(1)} %get-tuple-element.27), channel_id=1, source_target_pairs={{64,128},{128,64},{65,129},{129,65},{66,130},{130,66},{67,131},{13... | collective-permute-start | bytes 36872 | tf_op jit(solution)/shard_map/ppermute | solution.py:471
  10.1 2.8 %shard_map.40 = (f32[2,10,48,128]{3,2,1,0:T(8,128)S(1)}, f32[10,48,128]{2,1,0:T(8,128)S(1)}, f32[2,10,48,128]{3,2,1,0:T(8,128)S(1)}, f32[2,7,32,128]{3,2,1,0:T(8,128)S(1)}, f32[1,5,32,128]{3,2,1,0:T(8,128)S(1)}) custom-call(f32[16,64,1024]{2,1,0:T(8,128)S(1)} %copy-done, ...), custom_call_target="tpu_custom_call", output_to_operand_aliasing={{0}: (3, {}), {1}: (4, {})} | custom-call | flops 5000000000 | bytes 2097152 | tf_op jit(solution)/shard_map/pallas_call | solution.py:475
  12.8 0.0 collective-permute-done.pa
  12.9 0.0 collective-permute-done.1.pb
  12.9 0.3 shard_map.41
  13.1 1.1 %collective-permute-start.2 = (f32[80,128]{1,0:T(8,128)S(1)}, f32[80,128]{1,0:T(8,128)S(1)}, u32[]{:S(2)}, u32[]{:S(2)}) collective-permute-start(f32[80,128]{1,0:T(8,128)S(1)} %get-tuple-element.35), channel_id=1, source_target_pairs={{0,16},{16,0},{32,48},{48,32},{1,17},{17,1},{33,49},{49,33},{2,18}... | collective-permute-start | bytes 122888 | tf_op jit(solution)/shard_map/ppermute | solution.py:471
  14.2 1.9 %collective-permute-start.3 = (f32[80,128]{1,0:T(8,128)S(1)}, f32[80,128]{1,0:T(8,128)S(1)}, u32[]{:S(2)}, u32[]{:S(2)}) collective-permute-start(f32[80,128]{1,0:T(8,128)S(1)} %get-tuple-element.36), channel_id=1, source_target_pairs={{16,32},{32,16},{17,33},{33,17},{18,34},{34,18},{19,35},{35,19},{2... | collective-permute-start | bytes 122888 | tf_op jit(solution)/shard_map/ppermute | solution.py:471
  16.1 0.0 collective-permute-done.2.pa
  16.1 2.8 %collective-permute-done.3.pb = f32[80,128]{1,0:T(8,128)S(1)} collective-permute-done((f32[80,128]{1,0:T(8,128)S(1)}, f32[80,128]{1,0:T(8,128)S(1)}, u32[]{:S(2)}, u32[]{:S(2)}) %collective-permute-start.3) | collective-permute-done | bytes 40992 | tf_op jit(solution)/shard_map/ppermute | solution.py:471
  18.9 0.1 shard_map.42
  19.0 2.8 %collective-permute-start.4 = (f32[208,128]{1,0:T(8,128)S(1)}, f32[208,128]{1,0:T(8,128)S(1)}, u32[]{:S(2)}, u32[]{:S(2)}) collective-permute-start(f32[208,128]{1,0:T(8,128)S(1)} %get-tuple-element.41), channel_id=1, source_target_pairs={{0,1},{1,0},{2,3},{3,2},{4,5},{5,4},{6,7},{7,6},{8,9},{9,8},{10,11... | collective-permute-start | bytes 319496 | tf_op jit(solution)/shard_map/ppermute | solution.py:471
  21.8 2.5 %collective-permute-start.5 = (f32[208,128]{1,0:T(8,128)S(1)}, f32[208,128]{1,0:T(8,128)S(1)}, u32[]{:S(2)}, u32[]{:S(2)}) collective-permute-start(f32[208,128]{1,0:T(8,128)S(1)} %get-tuple-element.42), channel_id=1, source_target_pairs={{1,2},{2,1},{3,4},{4,3},{5,6},{6,5},{7,8},{8,7},{9,10},{10,9},{11,... | collective-permute-start | bytes 319496 | tf_op jit(solution)/shard_map/ppermute | solution.py:471
  24.4 0.8 %shard_map.43.one_in = f32[8,32,512]{2,1,0:T(8,128)} custom-call(f32[2,10,48,128]{3,2,1,0:T(8,128)S(1)} %get-tuple-element.43.ea, f32[2,10,48,128]{3,2,1,0:T(8,128)S(1)} %get-tuple-element.44.eb), custom_call_target="tpu_custom_call" | custom-call | flops 100000000 | bytes 1048576 | tf_op jit(solution)/shard_map/pallas_call | solution.py:475
  25.2 0.0 collective-permute-done.4.pa
  25.2 4.0 %collective-permute-done.5.pb = f32[208,128]{1,0:T(8,128)S(1)} collective-permute-done((f32[208,128]{1,0:T(8,128)S(1)}, f32[208,128]{1,0:T(8,128)S(1)}, u32[]{:S(2)}, u32[]{:S(2)}) %collective-permute-start.5) | collective-permute-done | bytes 106528 | tf_op jit(solution)/shard_map/ppermute | solution.py:471
  29.2 0.7 %shard_map.44 = (f32[8,32,512]{2,1,0:T(8,128)}, f32[4,16,256]{2,1,0:T(8,128)}, f32[2,8,128]{2,1,0:T(8,128)}) custom-call(f32[208,128]{1,0:T(8,128)S(1)} %collective-permute-done.4.pa, f32[208,128]{1,0:T(8,128)S(1)} %collective-permute-done.5.pb, f32[2,10,48,128]{3,2,1,0:T(8,128)S(1)} %get-tuple-element.43.ea, ...), custom_call_target="tpu_custom_call", output_to_operand_aliasing={{0}: (6, {})} | custom-call | flops 100000000 | bytes 1048576 | tf_op jit(solution)/shard_map/pallas_call | solution.py:475
Async XLA Ops:
  0.6 2.5 %copy-start = (f32[16,64,1024]{2,1,0:T(8,128)S(1)}, f32[16,64,1024]{2,1,0:T(8,128)}, u32[]{:S(2)}) copy-start(f32[16,64,1024]{2,1,0:T(8,128)} %volume.5) | copy-start | bytes 12582916
  2.7 10.2 %collective-permute-start = (f32[24,128]{1,0:T(8,128)S(1)}, f32[24,128]{1,0:T(8,128)S(1)}, u32[]{:S(2)}, u32[]{:S(2)}) collective-permute-start(f32[24,128]{1,0:T(8,128)S(1)} %get-tuple-element.25.shells), channel_id=1, source_target_pairs={{0,64},{64,0},{128,192},{192,128},{1,65},{65,1},{129,193},{193,129... | collective-permute-start | bytes 36872 | tf_op jit(solution)/shard_map/ppermute | solution.py:471
  4.6 8.3 %collective-permute-start.1 = (f32[24,128]{1,0:T(8,128)S(1)}, f32[24,128]{1,0:T(8,128)S(1)}, u32[]{:S(2)}, u32[]{:S(2)}) collective-permute-start(f32[24,128]{1,0:T(8,128)S(1)} %get-tuple-element.27), channel_id=1, source_target_pairs={{64,128},{128,64},{65,129},{129,65},{66,130},{130,66},{67,131},{13... | collective-permute-start | bytes 36872 | tf_op jit(solution)/shard_map/ppermute | solution.py:471
  13.1 3.0 %collective-permute-start.2 = (f32[80,128]{1,0:T(8,128)S(1)}, f32[80,128]{1,0:T(8,128)S(1)}, u32[]{:S(2)}, u32[]{:S(2)}) collective-permute-start(f32[80,128]{1,0:T(8,128)S(1)} %get-tuple-element.35), channel_id=1, source_target_pairs={{0,16},{16,0},{32,48},{48,32},{1,17},{17,1},{33,49},{49,33},{2,18}... | collective-permute-start | bytes 122888 | tf_op jit(solution)/shard_map/ppermute | solution.py:471
  14.2 4.7 %collective-permute-start.3 = (f32[80,128]{1,0:T(8,128)S(1)}, f32[80,128]{1,0:T(8,128)S(1)}, u32[]{:S(2)}, u32[]{:S(2)}) collective-permute-start(f32[80,128]{1,0:T(8,128)S(1)} %get-tuple-element.36), channel_id=1, source_target_pairs={{16,32},{32,16},{17,33},{33,17},{18,34},{34,18},{19,35},{35,19},{2... | collective-permute-start | bytes 122888 | tf_op jit(solution)/shard_map/ppermute | solution.py:471
  19.0 6.1 %collective-permute-start.4 = (f32[208,128]{1,0:T(8,128)S(1)}, f32[208,128]{1,0:T(8,128)S(1)}, u32[]{:S(2)}, u32[]{:S(2)}) collective-permute-start(f32[208,128]{1,0:T(8,128)S(1)} %get-tuple-element.41), channel_id=1, source_target_pairs={{0,1},{1,0},{2,3},{3,2},{4,5},{5,4},{6,7},{7,6},{8,9},{9,8},{10,11... | collective-permute-start | bytes 319496 | tf_op jit(solution)/shard_map/ppermute | solution.py:471
  21.8 7.4 %collective-permute-start.5 = (f32[208,128]{1,0:T(8,128)S(1)}, f32[208,128]{1,0:T(8,128)S(1)}, u32[]{:S(2)}, u32[]{:S(2)}) collective-permute-start(f32[208,128]{1,0:T(8,128)S(1)} %get-tuple-element.42), channel_id=1, source_target_pairs={{1,2},{2,1},{3,4},{4,3},{5,6},{6,5},{7,8},{8,7},{9,10},{10,9},{11,... | collective-permute-start | bytes 319496 | tf_op jit(solution)/shard_map/ppermute | solution.py:471

commit v6 on v5

--- a/solution.py
+++ b/solution.py
@@ -101,20 +101,24 @@
         store(i, v)
 
 
-def rows(src, dst, at, half, ends):
+def rows(src, dst, at, half, above, ends):
     n = 2 * half
     dst[at, 8 : 8 + half, :] = weigh(
         [src[at, pl.ds(6 + k, half, stride=2), :] for k in range(5)]
     )
-    low = taps[3] * src[at, 7:8, :] + taps[4] * src[at, 8:9, :]
+    low = taps[4] * src[at, 8:9, :]
+    if above > 1:
+        low = low + taps[3] * src[at, 7:8, :]
     dst[at, 0:8, :] = jnp.where(
         lax.broadcasted_iota(jnp.int32, (8, 128), 0) == 7, low * ends[0], 0.0
     )
-    up = [src[at, 6 + n + k : 7 + n + k, :] for k in range(4)]
-    high = weigh(up + [None]) * ends[1]
-    higher = (taps[0] * up[2] + taps[1] * up[3]) * ends[1]
+    up = [src[at, 6 + n + k : 7 + n + k, :] for k in range(2 * above)]
+    high = weigh((up + [None] * 4)[:5]) * ends[1]
     row = lax.broadcasted_iota(jnp.int32, (8, 128), 0)
-    dst[at, 8 + half : 16 + half, :] = jnp.where(row == 0, high, jnp.where(row == 1, higher, 0.0))
+    tile = jnp.where(row == 0, high, 0.0)
+    if above > 1:
+        tile = jnp.where(row == 1, (taps[0] * up[2] + taps[1] * up[3]) * ends[1], tile)
+    dst[at, 8 + half : 16 + half, :] = tile
 
 
 def pack(parts, dst, at):
@@ -146,7 +150,7 @@
 
         sections(lambda i, r=r: src[i, r : r + 8, :], store, 0, 15, 8, 1, zend)
     for s in range(10):
-        rows(z1, y1, s, 32, yend)
+        rows(z1, y1, s, 32, 1, yend)
     for a, zb, b, used, first, half_z, half_y in (
         (y1, z2, y2, 48, 8, 4, 16),
         (y2, z3, y3, 32, 5, 2, 8),
@@ -158,7 +162,7 @@
 
             sections(lambda i, r=r, a=a: a[i + 1, r : r + 8, :], store, -1, first, half_z, 2, zend)
         for s in range(half_z + 3):
-            rows(zb, b, s, half_y, yend)
+            rows(zb, b, s, half_y, 2, yend)
 
 
 TALL = ((0, 10, 48), (480, 7, 32), (704, 5, 32))
@@ -209,7 +213,7 @@
 def level_one_block(volume, at, zs, ys, ops, res, w, zend, yend):
     for h in range(2):
         cols = pl.ds(at * 256 + h * 128, 128)
-        for s in range(10):
+        for s in range(10 if at % 2 == 0 else 0):
             zs[h, s, 0:8, :] = jnp.zeros((8, 128), f32)
             zs[h, s, 72:80, :] = jnp.zeros((8, 128), f32)
         for r in range(0, 64, 8):
@@ -220,7 +224,7 @@
             sections(lambda i, r=r, cols=cols: volume[i, r : r + 8, cols], store, 0, 15, 8, 1, zend)
     for s in range(10):
         for h in range(2):
-            rows(zs.at[h], ys.at[h], s, 32, yend)
+            rows(zs.at[h], ys.at[h], s, 32, 1, yend)
         pack([ys[0, s], ys[1, s]], ops, s * 48)
     res[...] = matmul(ops[...], w[...])
 
@@ -268,7 +272,7 @@
             sections(lambda i, r=r, src=src: src[i + 1, r : r + 8, :], store, -1,
                      sections_in - 2, half_z, 2, zend)
         for s in range(many):
-            rows(zs.at[j], ys.at[j], s, half_y, yend)
+            rows(zs.at[j], ys.at[j], s, half_y, 2, yend)
     size = many * tall
     for p in range(count // 2):
         for s in range(many):

time: 30.1 us -> 30 us (level)
  transfers between devices with their start and end apart: 6 -> 6, of which waited for: 2 -> 2; matrix products, arithmetic and copies ran while one was open for 0% -> 0% of each run, Pallas kernels for 17% -> 16%
where the time goes in v6:
time: 30 us; the launch traced here: 29.9 us
  starting transfers between devices  13.9 us (46%)
  Pallas kernels  7.99 us (27%)
  waiting for transfers between devices  6.86 us (23%)
  between operations  0.75 us (2%)
  local copies, waits for them, and re-layouts  0.36 us (1%)
    ppermute x6, starting transfers between devices, swap(): return lax.ppermute(x, axis, pairs)  13.9 us
    pallas_call x7, Pallas kernels, call(): pl.pallas_call(kernel, out_shape=outs, in_specs=specs or [VMEM] * len(arg...  7.99 us
    ppermute x6, waiting for transfers between devices, swap(): return lax.ppermute(x, axis, pairs)  6.86 us
  transfers between devices with their start and end apart: 6, of which 2 were waited for; matrix products, arithmetic and copies ran while one was open for 0% of the time, Pallas kernels for 16%

profile of v6, /device:TPU:85, one launch (start us, length us, event | category | flops | bytes accessed | tf_op | source)
XLA Modules:
  0.0 29.9 jit_solution(13517069962256329292)
XLA Ops:
  0.6 0.0 copy-start
  0.6 2.0 %shard_map.38 = (f32[24,128]{1,0:T(8,128)S(1)}, bf16[768,256]{1,0:T(8,128)(2,1)S(1)}, bf16[384,256]{1,0:T(8,128)(2,1)S(1)}) custom-call(f32[16,64,1024]{2,1,0:T(8,128)} %volume.5), custom_call_target="tpu_custom_call" | custom-call | flops 100000000 | bytes 1048576 | tf_op jit(solution)/shard_map/pallas_call | solution.py:479
  2.7 0.1 collective-permute-start
  2.8 0.4 %copy-done = f32[16,64,1024]{2,1,0:T(8,128)S(1)} copy-done((f32[16,64,1024]{2,1,0:T(8,128)S(1)}, f32[16,64,1024]{2,1,0:T(8,128)}, u32[]{:S(2)}) %copy-start) | copy-done | bytes 4194328
  3.1 1.4 %shard_map.39 = (f32[2,10,48,128]{3,2,1,0:T(8,128)S(1)}, f32[10,48,128]{2,1,0:T(8,128)S(1)}, f32[24,128]{1,0:T(8,128)S(1)}) custom-call(f32[16,64,1024]{2,1,0:T(8,128)S(1)} %copy-done, bf16[768,256]{1,0:T(8,128)(2,1)S(1)} %get-tuple-element.26.w, f32[24,128]{1,0:T(8,128)S(1)} %get-tuple-element.25.shells), custom_call_target="tpu_custom_call" | custom-call | flops 4000000000 | bytes 2097152 | tf_op jit(solution)/shard_map/pallas_call | solution.py:479
  4.5 5.5 %collective-permute-start.1 = (f32[24,128]{1,0:T(8,128)S(1)}, f32[24,128]{1,0:T(8,128)S(1)}, u32[]{:S(2)}, u32[]{:S(2)}) collective-permute-start(f32[24,128]{1,0:T(8,128)S(1)} %get-tuple-element.27), channel_id=1, source_target_pairs={{64,128},{128,64},{65,129},{129,65},{66,130},{130,66},{67,131},{13... | collective-permute-start | bytes 36872 | tf_op jit(solution)/shard_map/ppermute | solution.py:475
  10.1 2.7 %shard_map.40 = (f32[2,10,48,128]{3,2,1,0:T(8,128)S(1)}, f32[10,48,128]{2,1,0:T(8,128)S(1)}, f32[2,10,48,128]{3,2,1,0:T(8,128)S(1)}, f32[2,7,32,128]{3,2,1,0:T(8,128)S(1)}, f32[1,5,32,128]{3,2,1,0:T(8,128)S(1)}) custom-call(f32[16,64,1024]{2,1,0:T(8,128)S(1)} %copy-done, ...), custom_call_target="tpu_custom_call", output_to_operand_aliasing={{0}: (3, {}), {1}: (4, {})} | custom-call | flops 5000000000 | bytes 2097152 | tf_op jit(solution)/shard_map/pallas_call | solution.py:479
  12.8 0.0 collective-permute-done.pa
  12.8 0.0 collective-permute-done.1.pb
  12.8 0.3 shard_map.41
  13.1 1.1 %collective-permute-start.2 = (f32[80,128]{1,0:T(8,128)S(1)}, f32[80,128]{1,0:T(8,128)S(1)}, u32[]{:S(2)}, u32[]{:S(2)}) collective-permute-start(f32[80,128]{1,0:T(8,128)S(1)} %get-tuple-element.35), channel_id=1, source_target_pairs={{0,16},{16,0},{32,48},{48,32},{1,17},{17,1},{33,49},{49,33},{2,18}... | collective-permute-start | bytes 122888 | tf_op jit(solution)/shard_map/ppermute | solution.py:475
  14.1 1.9 %collective-permute-start.3 = (f32[80,128]{1,0:T(8,128)S(1)}, f32[80,128]{1,0:T(8,128)S(1)}, u32[]{:S(2)}, u32[]{:S(2)}) collective-permute-start(f32[80,128]{1,0:T(8,128)S(1)} %get-tuple-element.36), channel_id=1, source_target_pairs={{16,32},{32,16},{17,33},{33,17},{18,34},{34,18},{19,35},{35,19},{2... | collective-permute-start | bytes 122888 | tf_op jit(solution)/shard_map/ppermute | solution.py:475
  16.0 0.0 collective-permute-done.2.pa
  16.0 2.8 %collective-permute-done.3.pb = f32[80,128]{1,0:T(8,128)S(1)} collective-permute-done((f32[80,128]{1,0:T(8,128)S(1)}, f32[80,128]{1,0:T(8,128)S(1)}, u32[]{:S(2)}, u32[]{:S(2)}) %collective-permute-start.3) | collective-permute-done | bytes 40992 | tf_op jit(solution)/shard_map/ppermute | solution.py:475
  18.9 0.1 shard_map.42
  19.0 2.8 %collective-permute-start.4 = (f32[208,128]{1,0:T(8,128)S(1)}, f32[208,128]{1,0:T(8,128)S(1)}, u32[]{:S(2)}, u32[]{:S(2)}) collective-permute-start(f32[208,128]{1,0:T(8,128)S(1)} %get-tuple-element.41), channel_id=1, source_target_pairs={{0,1},{1,0},{2,3},{3,2},{4,5},{5,4},{6,7},{7,6},{8,9},{9,8},{10,11... | collective-permute-start | bytes 319496 | tf_op jit(solution)/shard_map/ppermute | solution.py:475
  21.7 2.5 %collective-permute-start.5 = (f32[208,128]{1,0:T(8,128)S(1)}, f32[208,128]{1,0:T(8,128)S(1)}, u32[]{:S(2)}, u32[]{:S(2)}) collective-permute-start(f32[208,128]{1,0:T(8,128)S(1)} %get-tuple-element.42), channel_id=1, source_target_pairs={{1,2},{2,1},{3,4},{4,3},{5,6},{6,5},{7,8},{8,7},{9,10},{10,9},{11,... | collective-permute-start | bytes 319496 | tf_op jit(solution)/shard_map/ppermute | solution.py:475
  24.3 0.8 %shard_map.43.one_in = f32[8,32,512]{2,1,0:T(8,128)} custom-call(f32[2,10,48,128]{3,2,1,0:T(8,128)S(1)} %get-tuple-element.43.ea, f32[2,10,48,128]{3,2,1,0:T(8,128)S(1)} %get-tuple-element.44.eb), custom_call_target="tpu_custom_call" | custom-call | flops 100000000 | bytes 1048576 | tf_op jit(solution)/shard_map/pallas_call | solution.py:479
  25.1 0.0 collective-permute-done.4.pa
  25.1 4.0 %collective-permute-done.5.pb = f32[208,128]{1,0:T(8,128)S(1)} collective-permute-done((f32[208,128]{1,0:T(8,128)S(1)}, f32[208,128]{1,0:T(8,128)S(1)}, u32[]{:S(2)}, u32[]{:S(2)}) %collective-permute-start.5) | collective-permute-done | bytes 106528 | tf_op jit(solution)/shard_map/ppermute | solution.py:475
  29.1 0.7 %shard_map.44 = (f32[8,32,512]{2,1,0:T(8,128)}, f32[4,16,256]{2,1,0:T(8,128)}, f32[2,8,128]{2,1,0:T(8,128)}) custom-call(f32[208,128]{1,0:T(8,128)S(1)} %collective-permute-done.4.pa, f32[208,128]{1,0:T(8,128)S(1)} %collective-permute-done.5.pb, f32[2,10,48,128]{3,2,1,0:T(8,128)S(1)} %get-tuple-element.43.ea, ...), custom_call_target="tpu_custom_call", output_to_operand_aliasing={{0}: (6, {})} | custom-call | flops 100000000 | bytes 1048576 | tf_op jit(solution)/shard_map/pallas_call | solution.py:479
Async XLA Ops:
  0.6 2.5 %copy-start = (f32[16,64,1024]{2,1,0:T(8,128)S(1)}, f32[16,64,1024]{2,1,0:T(8,128)}, u32[]{:S(2)}) copy-start(f32[16,64,1024]{2,1,0:T(8,128)} %volume.5) | copy-start | bytes 12582916
  2.7 10.1 %collective-permute-start = (f32[24,128]{1,0:T(8,128)S(1)}, f32[24,128]{1,0:T(8,128)S(1)}, u32[]{:S(2)}, u32[]{:S(2)}) collective-permute-start(f32[24,128]{1,0:T(8,128)S(1)} %get-tuple-element.25.shells), channel_id=1, source_target_pairs={{0,64},{64,0},{128,192},{192,128},{1,65},{65,1},{129,193},{193,129... | collective-permute-start | bytes 36872 | tf_op jit(solution)/shard_map/ppermute | solution.py:475
  4.5 8.2 %collective-permute-start.1 = (f32[24,128]{1,0:T(8,128)S(1)}, f32[24,128]{1,0:T(8,128)S(1)}, u32[]{:S(2)}, u32[]{:S(2)}) collective-permute-start(f32[24,128]{1,0:T(8,128)S(1)} %get-tuple-element.27), channel_id=1, source_target_pairs={{64,128},{128,64},{65,129},{129,65},{66,130},{130,66},{67,131},{13... | collective-permute-start | bytes 36872 | tf_op jit(solution)/shard_map/ppermute | solution.py:475
  13.1 3.0 %collective-permute-start.2 = (f32[80,128]{1,0:T(8,128)S(1)}, f32[80,128]{1,0:T(8,128)S(1)}, u32[]{:S(2)}, u32[]{:S(2)}) collective-permute-start(f32[80,128]{1,0:T(8,128)S(1)} %get-tuple-element.35), channel_id=1, source_target_pairs={{0,16},{16,0},{32,48},{48,32},{1,17},{17,1},{33,49},{49,33},{2,18}... | collective-permute-start | bytes 122888 | tf_op jit(solution)/shard_map/ppermute | solution.py:475
  14.1 4.7 %collective-permute-start.3 = (f32[80,128]{1,0:T(8,128)S(1)}, f32[80,128]{1,0:T(8,128)S(1)}, u32[]{:S(2)}, u32[]{:S(2)}) collective-permute-start(f32[80,128]{1,0:T(8,128)S(1)} %get-tuple-element.36), channel_id=1, source_target_pairs={{16,32},{32,16},{17,33},{33,17},{18,34},{34,18},{19,35},{35,19},{2... | collective-permute-start | bytes 122888 | tf_op jit(solution)/shard_map/ppermute | solution.py:475
  19.0 6.1 %collective-permute-start.4 = (f32[208,128]{1,0:T(8,128)S(1)}, f32[208,128]{1,0:T(8,128)S(1)}, u32[]{:S(2)}, u32[]{:S(2)}) collective-permute-start(f32[208,128]{1,0:T(8,128)S(1)} %get-tuple-element.41), channel_id=1, source_target_pairs={{0,1},{1,0},{2,3},{3,2},{4,5},{5,4},{6,7},{7,6},{8,9},{9,8},{10,11... | collective-permute-start | bytes 319496 | tf_op jit(solution)/shard_map/ppermute | solution.py:475
  21.7 7.4 %collective-permute-start.5 = (f32[208,128]{1,0:T(8,128)S(1)}, f32[208,128]{1,0:T(8,128)S(1)}, u32[]{:S(2)}, u32[]{:S(2)}) collective-permute-start(f32[208,128]{1,0:T(8,128)S(1)} %get-tuple-element.42), channel_id=1, source_target_pairs={{1,2},{2,1},{3,4},{4,3},{5,6},{6,5},{7,8},{8,7},{9,10},{10,9},{11,... | collective-permute-start | bytes 319496 | tf_op jit(solution)/shard_map/ppermute | solution.py:475

commit v7 on v6

--- a/solution.py
+++ b/solution.py
@@ -171,8 +171,11 @@
 
 def shell_kernel(volume, out, reduce_w, wrap_w, left, right, own, w, lines, prod, z1, z2, z3, flat, sems):
     copies = []
-    for j, (first, dst) in enumerate(((0, left), (896, right))):
-        copies.append(pltpu.make_async_copy(volume.at[:, :, pl.ds(first, 128)], dst, sems.at[j]))
+    for j in range(4):
+        first, dst, part = (0, 896)[j % 2], (left, right)[j % 2], pl.ds(j // 2 * 8, 8)
+        copies.append(
+            pltpu.make_async_copy(volume.at[part, :, pl.ds(first, 128)], dst.at[part], sems.at[j])
+        )
     for c in copies:
         c.start()
     zend, yend = keep("gz", lax.axis_size("gz")), keep("gy", lax.axis_size("gy"))
@@ -186,10 +189,11 @@
         flat[704 + s * 32 + 24 : 704 + s * 32 + 32, :] = jnp.zeros((8, 128), f32)
     flat[864:896, :] = jnp.zeros((32, 128), f32)
     out[16:24, :] = jnp.zeros((8, 128), f32)
-    copies[0].wait()
-    copies[1].wait()
     low = low_lanes(64)
     for s in range(16):
+        if s % 8 == 0:
+            copies[s // 4].wait()
+            copies[s // 4 + 1].wait()
         pack([jnp.where(low, left[s], right[s])], lines, s * 64)
     prod[...] = matmul(lines[...], w[...])
     for s in range(16):
@@ -497,7 +501,7 @@
         [buf((16, 64, 128), f32)] * 3
         + [buf((384, 256), bf16), buf((1024, 384), bf16), buf((1024, 256), f32)]
         + levels
-        + [buf((896, 128), f32), pltpu.SemaphoreType.DMA((2,))],
+        + [buf((896, 128), f32), pltpu.SemaphoreType.DMA((4,))],
         (volume,),
         10**8,
         1 << 20,

time: 30 us -> 30 us (level)
  no operation moved by 1% of the time
where the time goes in v7:
time: 30 us; the launch traced here: 29.9 us
  starting transfers between devices  13.9 us (46%)
  Pallas kernels  7.98 us (27%)
  waiting for transfers between devices  6.86 us (23%)
  between operations  0.75 us (2%)
  local copies, waits for them, and re-layouts  0.37 us (1%)
    ppermute x6, starting transfers between devices, swap(): return lax.ppermute(x, axis, pairs)  13.9 us
    pallas_call x7, Pallas kernels, call(): pl.pallas_call(kernel, out_shape=outs, in_specs=specs or [VMEM] * len(arg...  7.98 us
    ppermute x6, waiting for transfers between devices, swap(): return lax.ppermute(x, axis, pairs)  6.86 us
  transfers between devices with their start and end apart: 6, of which 2 were waited for; matrix products, arithmetic and copies ran while one was open for 0% of the time, Pallas kernels for 16%

profile of v7, /device:TPU:85, one launch (start us, length us, event | category | flops | bytes accessed | tf_op | source)
XLA Modules:
  0.0 29.9 jit_solution(17936731443552344197)
XLA Ops:
  0.6 0.0 copy-start
  0.6 2.0 %shard_map.38 = (f32[24,128]{1,0:T(8,128)S(1)}, bf16[768,256]{1,0:T(8,128)(2,1)S(1)}, bf16[384,256]{1,0:T(8,128)(2,1)S(1)}) custom-call(f32[16,64,1024]{2,1,0:T(8,128)} %volume.5), custom_call_target="tpu_custom_call" | custom-call | flops 100000000 | bytes 1048576 | tf_op jit(solution)/shard_map/pallas_call | solution.py:483
  2.7 0.1 collective-permute-start
  2.8 0.4 %copy-done = f32[16,64,1024]{2,1,0:T(8,128)S(1)} copy-done((f32[16,64,1024]{2,1,0:T(8,128)S(1)}, f32[16,64,1024]{2,1,0:T(8,128)}, u32[]{:S(2)}) %copy-start) | copy-done | bytes 4194328
  3.1 1.4 %shard_map.39 = (f32[2,10,48,128]{3,2,1,0:T(8,128)S(1)}, f32[10,48,128]{2,1,0:T(8,128)S(1)}, f32[24,128]{1,0:T(8,128)S(1)}) custom-call(f32[16,64,1024]{2,1,0:T(8,128)S(1)} %copy-done, bf16[768,256]{1,0:T(8,128)(2,1)S(1)} %get-tuple-element.26.w, f32[24,128]{1,0:T(8,128)S(1)} %get-tuple-element.25.shells), custom_call_target="tpu_custom_call" | custom-call | flops 4000000000 | bytes 2097152 | tf_op jit(solution)/shard_map/pallas_call | solution.py:483
  4.5 5.5 %collective-permute-start.1 = (f32[24,128]{1,0:T(8,128)S(1)}, f32[24,128]{1,0:T(8,128)S(1)}, u32[]{:S(2)}, u32[]{:S(2)}) collective-permute-start(f32[24,128]{1,0:T(8,128)S(1)} %get-tuple-element.27), channel_id=1, source_target_pairs={{64,128},{128,64},{65,129},{129,65},{66,130},{130,66},{67,131},{13... | collective-permute-start | bytes 36872 | tf_op jit(solution)/shard_map/ppermute | solution.py:479
  10.1 2.7 %shard_map.40 = (f32[2,10,48,128]{3,2,1,0:T(8,128)S(1)}, f32[10,48,128]{2,1,0:T(8,128)S(1)}, f32[2,10,48,128]{3,2,1,0:T(8,128)S(1)}, f32[2,7,32,128]{3,2,1,0:T(8,128)S(1)}, f32[1,5,32,128]{3,2,1,0:T(8,128)S(1)}) custom-call(f32[16,64,1024]{2,1,0:T(8,128)S(1)} %copy-done, ...), custom_call_target="tpu_custom_call", output_to_operand_aliasing={{0}: (3, {}), {1}: (4, {})} | custom-call | flops 5000000000 | bytes 2097152 | tf_op jit(solution)/shard_map/pallas_call | solution.py:483
  12.7 0.0 collective-permute-done.pa
  12.8 0.0 collective-permute-done.1.pb
  12.8 0.3 shard_map.41
  13.0 1.1 %collective-permute-start.2 = (f32[80,128]{1,0:T(8,128)S(1)}, f32[80,128]{1,0:T(8,128)S(1)}, u32[]{:S(2)}, u32[]{:S(2)}) collective-permute-start(f32[80,128]{1,0:T(8,128)S(1)} %get-tuple-element.35), channel_id=1, source_target_pairs={{0,16},{16,0},{32,48},{48,32},{1,17},{17,1},{33,49},{49,33},{2,18}... | collective-permute-start | bytes 122888 | tf_op jit(solution)/shard_map/ppermute | solution.py:479
  14.1 1.9 %collective-permute-start.3 = (f32[80,128]{1,0:T(8,128)S(1)}, f32[80,128]{1,0:T(8,128)S(1)}, u32[]{:S(2)}, u32[]{:S(2)}) collective-permute-start(f32[80,128]{1,0:T(8,128)S(1)} %get-tuple-element.36), channel_id=1, source_target_pairs={{16,32},{32,16},{17,33},{33,17},{18,34},{34,18},{19,35},{35,19},{2... | collective-permute-start | bytes 122888 | tf_op jit(solution)/shard_map/ppermute | solution.py:479
  16.0 0.0 collective-permute-done.2.pa
  16.0 2.8 %collective-permute-done.3.pb = f32[80,128]{1,0:T(8,128)S(1)} collective-permute-done((f32[80,128]{1,0:T(8,128)S(1)}, f32[80,128]{1,0:T(8,128)S(1)}, u32[]{:S(2)}, u32[]{:S(2)}) %collective-permute-start.3) | collective-permute-done | bytes 40992 | tf_op jit(solution)/shard_map/ppermute | solution.py:479
  18.8 0.1 shard_map.42
  19.0 2.8 %collective-permute-start.4 = (f32[208,128]{1,0:T(8,128)S(1)}, f32[208,128]{1,0:T(8,128)S(1)}, u32[]{:S(2)}, u32[]{:S(2)}) collective-permute-start(f32[208,128]{1,0:T(8,128)S(1)} %get-tuple-element.41), channel_id=1, source_target_pairs={{0,1},{1,0},{2,3},{3,2},{4,5},{5,4},{6,7},{7,6},{8,9},{9,8},{10,11... | collective-permute-start | bytes 319496 | tf_op jit(solution)/shard_map/ppermute | solution.py:479
  21.7 2.5 %collective-permute-start.5 = (f32[208,128]{1,0:T(8,128)S(1)}, f32[208,128]{1,0:T(8,128)S(1)}, u32[]{:S(2)}, u32[]{:S(2)}) collective-permute-start(f32[208,128]{1,0:T(8,128)S(1)} %get-tuple-element.42), channel_id=1, source_target_pairs={{1,2},{2,1},{3,4},{4,3},{5,6},{6,5},{7,8},{8,7},{9,10},{10,9},{11,... | collective-permute-start | bytes 319496 | tf_op jit(solution)/shard_map/ppermute | solution.py:479
  24.3 0.8 %shard_map.43.one_in = f32[8,32,512]{2,1,0:T(8,128)} custom-call(f32[2,10,48,128]{3,2,1,0:T(8,128)S(1)} %get-tuple-element.43.ea, f32[2,10,48,128]{3,2,1,0:T(8,128)S(1)} %get-tuple-element.44.eb), custom_call_target="tpu_custom_call" | custom-call | flops 100000000 | bytes 1048576 | tf_op jit(solution)/shard_map/pallas_call | solution.py:483
  25.1 0.0 collective-permute-done.4.pa
  25.1 4.0 %collective-permute-done.5.pb = f32[208,128]{1,0:T(8,128)S(1)} collective-permute-done((f32[208,128]{1,0:T(8,128)S(1)}, f32[208,128]{1,0:T(8,128)S(1)}, u32[]{:S(2)}, u32[]{:S(2)}) %collective-permute-start.5) | collective-permute-done | bytes 106528 | tf_op jit(solution)/shard_map/ppermute | solution.py:479
  29.1 0.7 %shard_map.44 = (f32[8,32,512]{2,1,0:T(8,128)}, f32[4,16,256]{2,1,0:T(8,128)}, f32[2,8,128]{2,1,0:T(8,128)}) custom-call(f32[208,128]{1,0:T(8,128)S(1)} %collective-permute-done.4.pa, f32[208,128]{1,0:T(8,128)S(1)} %collective-permute-done.5.pb, f32[2,10,48,128]{3,2,1,0:T(8,128)S(1)} %get-tuple-element.43.ea, ...), custom_call_target="tpu_custom_call", output_to_operand_aliasing={{0}: (6, {})} | custom-call | flops 100000000 | bytes 1048576 | tf_op jit(solution)/shard_map/pallas_call | solution.py:483
Async XLA Ops:
  0.6 2.5 %copy-start = (f32[16,64,1024]{2,1,0:T(8,128)S(1)}, f32[16,64,1024]{2,1,0:T(8,128)}, u32[]{:S(2)}) copy-start(f32[16,64,1024]{2,1,0:T(8,128)} %volume.5) | copy-start | bytes 12582916
  2.7 10.1 %collective-permute-start = (f32[24,128]{1,0:T(8,128)S(1)}, f32[24,128]{1,0:T(8,128)S(1)}, u32[]{:S(2)}, u32[]{:S(2)}) collective-permute-start(f32[24,128]{1,0:T(8,128)S(1)} %get-tuple-element.25.shells), channel_id=1, source_target_pairs={{0,64},{64,0},{128,192},{192,128},{1,65},{65,1},{129,193},{193,129... | collective-permute-start | bytes 36872 | tf_op jit(solution)/shard_map/ppermute | solution.py:479
  4.5 8.2 %collective-permute-start.1 = (f32[24,128]{1,0:T(8,128)S(1)}, f32[24,128]{1,0:T(8,128)S(1)}, u32[]{:S(2)}, u32[]{:S(2)}) collective-permute-start(f32[24,128]{1,0:T(8,128)S(1)} %get-tuple-element.27), channel_id=1, source_target_pairs={{64,128},{128,64},{65,129},{129,65},{66,130},{130,66},{67,131},{13... | collective-permute-start | bytes 36872 | tf_op jit(solution)/shard_map/ppermute | solution.py:479
  13.0 3.0 %collective-permute-start.2 = (f32[80,128]{1,0:T(8,128)S(1)}, f32[80,128]{1,0:T(8,128)S(1)}, u32[]{:S(2)}, u32[]{:S(2)}) collective-permute-start(f32[80,128]{1,0:T(8,128)S(1)} %get-tuple-element.35), channel_id=1, source_target_pairs={{0,16},{16,0},{32,48},{48,32},{1,17},{17,1},{33,49},{49,33},{2,18}... | collective-permute-start | bytes 122888 | tf_op jit(solution)/shard_map/ppermute | solution.py:479
  14.1 4.7 %collective-permute-start.3 = (f32[80,128]{1,0:T(8,128)S(1)}, f32[80,128]{1,0:T(8,128)S(1)}, u32[]{:S(2)}, u32[]{:S(2)}) collective-permute-start(f32[80,128]{1,0:T(8,128)S(1)} %get-tuple-element.36), channel_id=1, source_target_pairs={{16,32},{32,16},{17,33},{33,17},{18,34},{34,18},{19,35},{35,19},{2... | collective-permute-start | bytes 122888 | tf_op jit(solution)/shard_map/ppermute | solution.py:479
  19.0 6.1 %collective-permute-start.4 = (f32[208,128]{1,0:T(8,128)S(1)}, f32[208,128]{1,0:T(8,128)S(1)}, u32[]{:S(2)}, u32[]{:S(2)}) collective-permute-start(f32[208,128]{1,0:T(8,128)S(1)} %get-tuple-element.41), channel_id=1, source_target_pairs={{0,1},{1,0},{2,3},{3,2},{4,5},{5,4},{6,7},{7,6},{8,9},{9,8},{10,11... | collective-permute-start | bytes 319496 | tf_op jit(solution)/shard_map/ppermute | solution.py:479
  21.7 7.4 %collective-permute-start.5 = (f32[208,128]{1,0:T(8,128)S(1)}, f32[208,128]{1,0:T(8,128)S(1)}, u32[]{:S(2)}, u32[]{:S(2)}) collective-permute-start(f32[208,128]{1,0:T(8,128)S(1)} %get-tuple-element.42), channel_id=1, source_target_pairs={{1,2},{2,1},{3,4},{4,3},{5,6},{6,5},{7,8},{8,7},{9,10},{10,9},{11,... | collective-permute-start | bytes 319496 | tf_op jit(solution)/shard_map/ppermute | solution.py:479
